TPU v7x, 256 devices: a whole 4x4x8 slice. The times are simulated.
256 devices in a mesh: row: 16 (over z, x_lo), col: 16 (over x_hi, y, core).
Axes of the slice: x: 4 (x_hi: 2, x_lo: 2; x = x_hi * 2 + x_lo), y: 4, z: 8, core: 2. Of those that a mesh axis runs over, the one named last changes fastest.
Arguments:
- tiles: bfloat16 [16, 16, 3, 256, 256], P('row', 'col'), as said below
- stack_index: int32 [16, 16, 3], P('row', 'col'), may hold values from 0 to 15, as said below
- block_mask: int32 [64, 64], replicated, may hold values from 0 to 1, as said below
Outputs:
- purified: bfloat16 [16, 16, 3, 256, 256], P('row', 'col')
Inputs may be any that keep to these rules, and one draw needn't show every extreme that they name: `block_mask`: the region of one device (4 x 4 blocks) holds at most 3 occupied blocks; some region holds exactly 3 in every draw. `stack_index`: block (a, b) of a device's region is numbered a * 4 + b. A device's 3 entries are distinct and include every occupied block of its region; a slot naming an unoccupied block holds a tile that P does not use. `tiles`: A slot's tile is P's block named by stack_index when that block is occupied.
All inputs are finite; a program needn't handle non-finite values.
Results may differ from a plain program's by a relative error of at most 0.0051.
Values may be sent and summed in bfloat16 or wider, within the bound.
A program may use at most 64 MiB of HBM per device.

v0:
```python
import jax
import jax.numpy as jnp
from jax import lax
from jax.sharding import PartitionSpec as P

NB = 64


def shortened(shard):

    def short(part):
        return part.astype(jnp.bfloat16) if part.dtype == jnp.float32 else part

    return jax.tree.map(short, shard)


def shifted(shard, axis, by):
    length = lax.axis_size(axis)
    return lax.ppermute(shard, axis, [(i, (i + by) % length) for i in range(length)])


def lookup_mask(mask_float, row_ids, col_ids):
    blocks = mask_float.shape[0]
    block_iota = jnp.arange(blocks, dtype=jnp.int32)
    row_hot = (row_ids[:, None] == block_iota[None, :]).astype(jnp.float32)
    col_hot = (col_ids[:, None] == block_iota[None, :]).astype(jnp.float32)
    picked = jnp.dot(row_hot, mask_float, precision=lax.Precision.HIGHEST)
    return jnp.sum(picked * col_hot, axis=1) > 0.5


def choose(flag, moved, held):
    return jax.tree.map(lambda first, second: jnp.where(flag, first, second), moved, held)


def contribution(
    left_pair, left_region, right_pair, right_region, own_labels, block_rows, block_cols
):
    left_tiles, left_labels = left_pair
    right_tiles, right_labels = right_pair
    slot_count = left_tiles.shape[0]
    side = left_tiles.shape[1]
    left_ids = left_labels.astype(jnp.int32)
    right_ids = right_labels.astype(jnp.int32)
    own_ids = own_labels.astype(jnp.int32)
    left_live = left_ids >= 0
    right_live = right_ids >= 0
    own_live = own_ids >= 0
    left_row = left_ids // block_cols
    left_inner = left_region * block_cols + left_ids % block_cols
    right_inner = right_region * block_rows + right_ids // block_cols
    right_col = right_ids % block_cols
    own_row = own_ids // block_cols
    own_col = own_ids % block_cols
    matched = own_live[:, None, None] & left_live[None, :, None] & right_live[None, None, :]
    matched = matched & (left_row[None, :, None] == own_row[:, None, None])
    matched = matched & (left_inner[None, :, None] == right_inner[None, None, :])
    matched = matched & (right_col[None, None, :] == own_col[:, None, None])
    matched_int = matched.astype(jnp.int32)
    right_places = jnp.arange(slot_count, dtype=jnp.int32)
    index = jnp.sum(matched_int * right_places[None, None, :], axis=2, dtype=jnp.int32)
    present = jnp.sum(matched_int, axis=2, dtype=jnp.int32)
    picked = jnp.take(right_tiles, index.reshape(slot_count * slot_count), axis=0)
    picked = (
        picked.reshape(slot_count, slot_count, side, side)
        * present.astype(jnp.bfloat16)[:, :, None, None]
    )
    return jnp.einsum("ixy,siyz->sxz", left_tiles, picked, preferred_element_type=jnp.float32)


def local(tiles, stack_index, block_mask):
    row_size = lax.axis_size("row")
    col_size = lax.axis_size("col")
    band_row = lax.axis_index("row")
    band_col = lax.axis_index("col")
    block_rows = NB // row_size
    block_cols = NB // col_size
    steps = max(row_size, col_size)
    left_group = steps // col_size
    right_group = steps // row_size
    mask_float = block_mask.astype(jnp.float32)
    own_ids = stack_index[0, 0]
    own_stack = tiles[0, 0]
    own_valid = lookup_mask(
        mask_float,
        band_row * block_rows + own_ids // block_cols,
        band_col * block_cols + own_ids % block_cols,
    )
    own_labels = jnp.where(own_valid, own_ids, -1).astype(jnp.bfloat16)
    left_offset = right_group * band_row // left_group % col_size
    right_offset = left_group * band_col // right_group % row_size
    left_start = (band_col + left_offset) % col_size
    right_start = (band_row + right_offset) % row_size
    panel_start = (left_group * band_col + right_group * band_row) % steps

    def skew_left(pair):
        for bit in range((col_size - 1).bit_length()):
            moved = jax.tree.map(
                lambda part, own: part.astype(own.dtype),
                shifted(shortened(pair), "col", -(1 << bit)),
                pair,
            )
            pair = choose(left_offset // (1 << bit) % 2 == 1, moved, pair)
        return pair

    def advance(carry_state, left_moved, right_moved, heading):
        left_pair, right_pair, left_region, right_region, panel = carry_state
        if heading > 0:
            take_left = (panel + 1) % left_group == 0
            take_right = (panel + 1) % right_group == 0
        else:
            take_left = panel % left_group == 0
            take_right = panel % right_group == 0
        left_pair = choose(take_left, left_moved, left_pair)
        right_pair = choose(take_right, right_moved, right_pair)
        left_region = jnp.where(take_left, (left_region + heading) % col_size, left_region)
        right_region = jnp.where(take_right, (right_region + heading) % row_size, right_region)
        panel = (panel + heading) % steps
        return (left_pair, right_pair, left_region, right_region, panel)

    def local_term(carry_state):
        return contribution(
            carry_state[0],
            carry_state[2],
            carry_state[1],
            carry_state[3],
            own_labels,
            block_rows,
            block_cols,
        )

    def multiply(left_pair, right_pair):
        start_state = (left_pair, right_pair, left_start, right_start, panel_start)
        total = local_term(start_state)

        def forward_turn(carry_state):
            left_moved = shifted(shortened(carry_state[0]), "col", -1)
            right_moved = shifted(shortened(carry_state[1]), "row", -1)
            return advance(carry_state, left_moved, right_moved, 1)

        def backward_turn(carry_state):
            left_moved = shifted(shortened(carry_state[0]), "col", 1)
            right_moved = shifted(shortened(carry_state[1]), "row", 1)
            return advance(carry_state, left_moved, right_moved, -1)

        backward_count = (steps - 1) // 2

        def paired_turn(turn_index, carry):
            running, ahead_state, behind_state = carry
            ahead_state = forward_turn(ahead_state)
            behind_state = backward_turn(behind_state)
            running = running + local_term(ahead_state) + local_term(behind_state)
            return (running, ahead_state, behind_state)

        total, ahead_state, behind_state = lax.fori_loop(
            0, backward_count, paired_turn, (total, start_state, start_state)
        )
        ahead_state = forward_turn(ahead_state)
        total = total + local_term(ahead_state)
        return total

    own_pair = (own_stack, own_labels)
    pair = own_pair
    for bit in range((row_size - 1).bit_length()):
        moved = jax.tree.map(
            lambda part, own: part.astype(own.dtype),
            shifted(shortened(pair), "row", -(1 << bit)),
            pair,
        )
        pair = choose(right_offset // (1 << bit) % 2 == 1, moved, pair)
    square = multiply(skew_left(own_pair), pair).astype(jnp.bfloat16)
    pair = own_pair
    for bit in range((row_size - 1).bit_length()):
        moved = jax.tree.map(
            lambda part, own: part.astype(own.dtype),
            shifted(shortened(pair), "row", -(1 << bit)),
            pair,
        )
        pair = choose(right_offset // (1 << bit) % 2 == 1, moved, pair)
    cube_sum = multiply(skew_left((square, own_labels)), pair)
    valid_float = own_valid.astype(jnp.float32)
    purified = (3.0 * square.astype(jnp.float32) - 2.0 * cube_sum) * valid_float[:, None, None]
    return purified.astype(jnp.bfloat16)[None, None]


def solution(mesh):
    placed = (P("row", "col", None, None, None), P("row", "col", None), P())
    return jax.shard_map(
        local,
        mesh=mesh,
        in_specs=placed,
        out_specs=P("row", "col", None, None, None),
        check_vma=False,
    )
```

profile of v0, /device:TPU:1, one launch (start us, length us, event | category | flops | bytes accessed | tf_op | source)
XLA Modules:
  0.0 713.4 jit_solution(5395732926060700012)
XLA Ops:
  1.2 7.4 %collective-permute-start.16 = (bf16[3,256,256]{1,2,0:T(8,128)(2,1)S(1)}, bf16[3,256,256]{1,2,0:T(8,128)(2,1)S(1)}, u32[]{:S(2)}, u32[]{:S(2)}) collective-permute-start(bf16[3,256,256]{1,2,0:T(8,128)(2,1)S(1)} %bitcast.133), channel_id=1, source_target_pairs={{0,240},{16,0},{32,16},{48,32},{64,48},{80,64},{96,80},{112,96},{1... | collective-permute-start | bytes 1179656 | tf_op jit(solution)/shard_map/ppermute | solution.py:19
  12.5 4.3 collective-permute-start.20
  20.2 4.9 collective-permute-start.21
  25.1 5.4 collective-permute-start.25
  39.4 3.9 collective-permute-done.27
  46.4 6.7 collective-permute-start.29
  56.9 4.2 collective-permute-done.29
  62.9 7.1 collective-permute-done.18
  70.1 3.5 collective-permute-done.30
  79.5 9.5 %collective-permute-done.19 = bf16[3,256,256]{1,2,0:T(8,128)(2,1)S(1)} collective-permute-done((bf16[3,256,256]{1,2,0:T(8,128)(2,1)S(1)}, bf16[3,256,256]{1,2,0:T(8,128)(2,1)S(1)}, u32[]{:S(2)}, u32[]{:S(2)}) %collective-permute-start.19) | collective-permute-done | bytes 393248 | tf_op jit(solution)/shard_map/ppermute | solution.py:19
  98.5 263.3 %while.78 = (s32[]{:T(128)}, f32[3,256,256]{1,2,0:T(8,128)}, bf16[3,256,256]{2,1,0:T(8,128)(2,1)}, bf16[3]{0:T(256)(128)(2,1)}, bf16[3,256,256]{2,1,0:T(8,128)(2...) while((s32[]{:T(128)}, f32[3,256,256]{1,2,0:T(8,128)}, ...), condition=%wide.region_8.10_spmd, body=%wide.region_3.9_spmd.sunk | while | flops 606735360 | bytes 40905304 | solution.py:154
  98.5 3.5 collective-permute-start.1
  102.0 4.7 collective-permute-start.4
  112.7 4.5 collective-permute-start.5
  119.2 5.0 collective-permute-start.7
  130.5 3.0 collective-permute-done.6
  144.3 2.9 collective-permute-start.4
  149.3 4.5 collective-permute-start.5
  156.4 6.5 collective-permute-start.7
  179.3 4.2 collective-permute-start.4
  185.6 4.5 collective-permute-start.5
  192.5 6.5 collective-permute-start.7
  215.3 5.8 collective-permute-start.4
  222.5 3.7 collective-permute-start.5
  229.2 6.5 collective-permute-start.7
  252.0 6.2 collective-permute-start.4
  266.3 6.5 collective-permute-start.7
  289.1 6.2 collective-permute-start.4
  298.2 3.6 collective-permute-done.3
  303.4 6.5 collective-permute-start.7
  326.2 6.2 collective-permute-start.4
  334.0 4.9 collective-permute-done.3
  340.5 6.5 collective-permute-start.7
  361.8 5.7 collective-permute-start.33
  367.5 3.0 collective-permute-start.32
  370.5 3.5 collective-permute-start.35
  379.6 5.1 collective-permute-start.36
  386.9 13.7 %collective-permute-start.37 = (bf16[3,256,256]{1,2,0:T(8,128)(2,1)S(1)}, bf16[3,256,256]{1,2,0:T(8,128)(2,1)S(1)}, u32[]{:S(2)}, u32[]{:S(2)}) collective-permute-start(bf16[3,256,256]{1,2,0:T(8,128)(2,1)S(1)} %broadcast_select_fusion.7), channel_id=1, source_target_pairs={{0,14},{1,15},{2,0},{3,1},{4,2},{5,3},{6,4},{7,5},{8,6},{9,7},{10,... | collective-permute-start | bytes 1179656 | tf_op jit(solution)/shard_map/ppermute | solution.py:19
  400.6 6.0 collective-permute-done.37
  407.1 9.1 %collective-permute-done.38 = bf16[3,256,256]{1,2,0:T(8,128)(2,1)S(1)} collective-permute-done((bf16[3,256,256]{1,2,0:T(8,128)(2,1)S(1)}, bf16[3,256,256]{1,2,0:T(8,128)(2,1)S(1)}, u32[]{:S(2)}, u32[]{:S(2)}) %collective-permute-start.38) | collective-permute-done | bytes 393248 | tf_op jit(solution)/shard_map/ppermute | solution.py:19
  416.2 11.8 %collective-permute-start.39 = (bf16[3,256,256]{1,2,0:T(8,128)(2,1)S(1)}, bf16[3,256,256]{1,2,0:T(8,128)(2,1)S(1)}, u32[]{:S(2)}, u32[]{:S(2)}) collective-permute-start(bf16[3,256,256]{1,2,0:T(8,128)(2,1)S(1)} %broadcast_select_fusion.11), channel_id=1, source_target_pairs={{0,8},{1,9},{2,10},{3,11},{4,12},{5,13},{6,14},{7,15},{8,0},{9,1},... | collective-permute-start | bytes 1179656 | tf_op jit(solution)/shard_map/ppermute | solution.py:19
  432.0 5.1 collective-permute-done.39
  441.4 252.8 %while.79 = (s32[]{:T(128)}, f32[3,256,256]{1,2,0:T(8,128)}, bf16[3,256,256]{2,1,0:T(8,128)(2,1)}, bf16[3]{0:T(256)(128)(2,1)}, bf16[3,256,256]{2,1,0:T(8,128)(2...) while((s32[]{:T(128)}, f32[3,256,256]{1,2,0:T(8,128)}, ...), condition=%wide.region_16.18_spmd, body=%wide.region_11.17_spmd.sunk | while | flops 606735360 | bytes 40905304 | solution.py:154
  451.2 6.2 collective-permute-start.15
  463.3 2.9 collective-permute-done.14
  476.5 4.9 collective-permute-start.12
  488.4 6.2 collective-permute-start.15
  512.9 3.9 collective-permute-start.12
  525.0 6.1 collective-permute-start.15
  547.3 6.6 collective-permute-start.12
  557.2 3.3 collective-permute-done.11
  562.1 6.2 collective-permute-start.15
  584.4 6.5 collective-permute-start.12
  593.1 4.5 collective-permute-done.11
  599.1 6.2 collective-permute-start.15
  621.5 6.5 collective-permute-start.12
  629.4 5.1 collective-permute-done.11
  636.2 6.2 collective-permute-start.15
  658.6 6.5 collective-permute-start.12
  666.5 5.1 collective-permute-done.11
  673.2 6.2 collective-permute-start.15
  694.2 6.0 collective-permute-start.41
  700.1 3.0 collective-permute-start.40
  703.1 3.5 collective-permute-start.43
  (1033 shorter events, 367.3 us)
Async XLA Ops:
  1.2 43.4 %collective-permute-start.16 = (bf16[3,256,256]{1,2,0:T(8,128)(2,1)S(1)}, bf16[3,256,256]{1,2,0:T(8,128)(2,1)S(1)}, u32[]{:S(2)}, u32[]{:S(2)}) collective-permute-start(bf16[3,256,256]{1,2,0:T(8,128)(2,1)S(1)} %bitcast.133), channel_id=1, source_target_pairs={{0,240},{16,0},{32,16},{48,32},{64,48},{80,64},{96,80},{112,96},{1... | collective-permute-start | bytes 1179656 | tf_op jit(solution)/shard_map/ppermute | solution.py:19
  8.6 36.0 %collective-permute-start.28 = (bf16[3,256,256]{1,2,0:T(8,128)(2,1)S(1)}, bf16[3,256,256]{1,2,0:T(8,128)(2,1)S(1)}, u32[]{:S(2)}, u32[]{:S(2)}) collective-permute-start(bf16[3,256,256]{1,2,0:T(8,128)(2,1)S(1)} %bitcast.134), channel_id=1, source_target_pairs={{0,15},{1,0},{2,1},{3,2},{4,3},{5,4},{6,5},{7,6},{8,7},{9,8},{10,9... | collective-permute-start | bytes 1179656 | tf_op jit(solution)/shard_map/ppermute | solution.py:19
  70.0 19.0 %collective-permute-start.19 = (bf16[3,256,256]{1,2,0:T(8,128)(2,1)S(1)}, bf16[3,256,256]{1,2,0:T(8,128)(2,1)S(1)}, u32[]{:S(2)}, u32[]{:S(2)}) collective-permute-start(bf16[3,256,256]{1,2,0:T(8,128)(2,1)S(1)} %broadcast_select_fusion.17), channel_id=1, source_target_pairs={{0,128},{16,144},{32,160},{48,176},{64,192},{80,208},{96,224},{112... | collective-permute-start | bytes 1179656 | tf_op jit(solution)/shard_map/ppermute | solution.py:19
  73.6 20.5 %collective-permute-start.31 = (bf16[3,256,256]{1,2,0:T(8,128)(2,1)S(1)}, bf16[3,256,256]{1,2,0:T(8,128)(2,1)S(1)}, u32[]{:S(2)}, u32[]{:S(2)}) collective-permute-start(bf16[3,256,256]{1,2,0:T(8,128)(2,1)S(1)} %broadcast_select_fusion.12), channel_id=1, source_target_pairs={{0,8},{1,9},{2,10},{3,11},{4,12},{5,13},{6,14},{7,15},{8,0},{9,1},... | collective-permute-start | bytes 1179656 | tf_op jit(solution)/shard_map/ppermute | solution.py:19
  98.5 20.7 %collective-permute-start.1 = (bf16[3]{0:T(256)(128)(2,1)}, bf16[3]{0:T(256)(128)(2,1)S(1)}, u32[]{:S(2)}, u32[]{:S(2)}) collective-permute-start(bf16[3]{0:T(256)(128)(2,1)} %get-tuple-element.1049), channel_id=1, source_target_pairs={{0,240},{16,0},{32,16},{48,32},{64,48},{80,64},{96,80},{112,96},{1... | collective-permute-start | bytes 26 | tf_op jit(solution)/shard_map/while/body/eval_jaxpr/ppermute | solution.py:19
  102.0 22.2 %collective-permute-start.4 = (bf16[3]{0:T(256)(128)(2,1)}, bf16[3]{0:T(256)(128)(2,1)S(1)}, u32[]{:S(2)}, u32[]{:S(2)}) collective-permute-start(bf16[3]{0:T(256)(128)(2,1)} %get-tuple-element.1047), channel_id=1, source_target_pairs={{0,15},{1,0},{2,1},{3,2},{4,3},{5,4},{6,5},{7,6},{8,7},{9,8},{10,9... | collective-permute-start | bytes 26 | tf_op jit(solution)/shard_map/while/body/eval_jaxpr/ppermute | solution.py:19
  109.2 18.9 %collective-permute-start = (bf16[3,256,256]{2,1,0:T(8,128)(2,1)}, bf16[3,256,256]{2,1,0:T(8,128)(2,1)S(1)}, u32[]{:S(2)}, u32[]{:S(2)}) collective-permute-start(bf16[3,256,256]{2,1,0:T(8,128)(2,1)} %get-tuple-element.1054), channel_id=1, source_target_pairs={{0,16},{16,32},{32,48},{48,64},{64,80},{80,96},{96,112},{112,128},... | collective-permute-start | bytes 1179656 | tf_op jit(solution)/shard_map/while/body/eval_jaxpr/ppermute | solution.py:19
  112.7 24.6 %collective-permute-start.5 = (bf16[3,256,256]{2,1,0:T(8,128)(2,1)}, bf16[3,256,256]{2,1,0:T(8,128)(2,1)}, u32[]{:S(2)}, u32[]{:S(2)}) collective-permute-start(bf16[3,256,256]{2,1,0:T(8,128)(2,1)} %get-tuple-element.1052), channel_id=1, source_target_pairs={{0,1},{1,2},{2,3},{3,4},{4,5},{5,6},{6,7},{7,8},{8,9},{9,10},{10,1... | collective-permute-start | bytes 1179656 | tf_op jit(solution)/shard_map/while/body/eval_jaxpr/ppermute | solution.py:19
  117.3 16.2 %collective-permute-start.6 = (bf16[3,256,256]{2,1,0:T(8,128)(2,1)}, bf16[3,256,256]{2,1,0:T(8,128)(2,1)S(1)}, u32[]{:S(2)}, u32[]{:S(2)}) collective-permute-start(bf16[3,256,256]{2,1,0:T(8,128)(2,1)} %get-tuple-element.1048), channel_id=1, source_target_pairs={{0,240},{16,0},{32,16},{48,32},{64,48},{80,64},{96,80},{112,96},{1... | collective-permute-start | bytes 1179656 | tf_op jit(solution)/shard_map/while/body/eval_jaxpr/ppermute | solution.py:19
  119.2 17.3 %collective-permute-start.7 = (bf16[3,256,256]{2,1,0:T(8,128)(2,1)}, bf16[3,256,256]{2,1,0:T(8,128)(2,1)S(1)}, u32[]{:S(2)}, u32[]{:S(2)}) collective-permute-start(bf16[3,256,256]{2,1,0:T(8,128)(2,1)} %get-tuple-element.1046), channel_id=1, source_target_pairs={{0,15},{1,0},{2,1},{3,2},{4,3},{5,4},{6,5},{7,6},{8,7},{9,8},{10,9... | collective-permute-start | bytes 1179656 | tf_op jit(solution)/shard_map/while/body/eval_jaxpr/ppermute | solution.py:19
  144.3 18.6 %collective-permute-start.4 = (bf16[3]{0:T(256)(128)(2,1)}, bf16[3]{0:T(256)(128)(2,1)S(1)}, u32[]{:S(2)}, u32[]{:S(2)}) collective-permute-start(bf16[3]{0:T(256)(128)(2,1)} %get-tuple-element.1047), channel_id=1, source_target_pairs={{0,15},{1,0},{2,1},{3,2},{4,3},{5,4},{6,5},{7,6},{8,7},{9,8},{10,9... | collective-permute-start | bytes 26 | tf_op jit(solution)/shard_map/while/body/eval_jaxpr/ppermute | solution.py:19
  147.9 18.6 %collective-permute-start = (bf16[3,256,256]{2,1,0:T(8,128)(2,1)}, bf16[3,256,256]{2,1,0:T(8,128)(2,1)S(1)}, u32[]{:S(2)}, u32[]{:S(2)}) collective-permute-start(bf16[3,256,256]{2,1,0:T(8,128)(2,1)} %get-tuple-element.1054), channel_id=1, source_target_pairs={{0,16},{16,32},{32,48},{48,64},{64,80},{80,96},{96,112},{112,128},... | collective-permute-start | bytes 1179656 | tf_op jit(solution)/shard_map/while/body/eval_jaxpr/ppermute | solution.py:19
  149.3 23.5 %collective-permute-start.5 = (bf16[3,256,256]{2,1,0:T(8,128)(2,1)}, bf16[3,256,256]{2,1,0:T(8,128)(2,1)}, u32[]{:S(2)}, u32[]{:S(2)}) collective-permute-start(bf16[3,256,256]{2,1,0:T(8,128)(2,1)} %get-tuple-element.1052), channel_id=1, source_target_pairs={{0,1},{1,2},{2,3},{3,4},{4,5},{5,6},{6,7},{7,8},{8,9},{9,10},{10,1... | collective-permute-start | bytes 1179656 | tf_op jit(solution)/shard_map/while/body/eval_jaxpr/ppermute | solution.py:19
  179.3 19.7 %collective-permute-start.4 = (bf16[3]{0:T(256)(128)(2,1)}, bf16[3]{0:T(256)(128)(2,1)S(1)}, u32[]{:S(2)}, u32[]{:S(2)}) collective-permute-start(bf16[3]{0:T(256)(128)(2,1)} %get-tuple-element.1047), channel_id=1, source_target_pairs={{0,15},{1,0},{2,1},{3,2},{4,3},{5,4},{6,5},{7,6},{8,7},{9,8},{10,9... | collective-permute-start | bytes 26 | tf_op jit(solution)/shard_map/while/body/eval_jaxpr/ppermute | solution.py:19
  184.2 18.4 %collective-permute-start = (bf16[3,256,256]{2,1,0:T(8,128)(2,1)}, bf16[3,256,256]{2,1,0:T(8,128)(2,1)S(1)}, u32[]{:S(2)}, u32[]{:S(2)}) collective-permute-start(bf16[3,256,256]{2,1,0:T(8,128)(2,1)} %get-tuple-element.1054), channel_id=1, source_target_pairs={{0,16},{16,32},{32,48},{48,64},{64,80},{80,96},{96,112},{112,128},... | collective-permute-start | bytes 1179656 | tf_op jit(solution)/shard_map/while/body/eval_jaxpr/ppermute | solution.py:19
  185.6 23.3 %collective-permute-start.5 = (bf16[3,256,256]{2,1,0:T(8,128)(2,1)}, bf16[3,256,256]{2,1,0:T(8,128)(2,1)}, u32[]{:S(2)}, u32[]{:S(2)}) collective-permute-start(bf16[3,256,256]{2,1,0:T(8,128)(2,1)} %get-tuple-element.1052), channel_id=1, source_target_pairs={{0,1},{1,2},{2,3},{3,4},{4,5},{5,6},{6,7},{7,8},{8,9},{9,10},{10,1... | collective-permute-start | bytes 1179656 | tf_op jit(solution)/shard_map/while/body/eval_jaxpr/ppermute | solution.py:19
  192.5 15.6 %collective-permute-start.7 = (bf16[3,256,256]{2,1,0:T(8,128)(2,1)}, bf16[3,256,256]{2,1,0:T(8,128)(2,1)S(1)}, u32[]{:S(2)}, u32[]{:S(2)}) collective-permute-start(bf16[3,256,256]{2,1,0:T(8,128)(2,1)} %get-tuple-element.1046), channel_id=1, source_target_pairs={{0,15},{1,0},{2,1},{3,2},{4,3},{5,4},{6,5},{7,6},{8,7},{9,8},{10,9... | collective-permute-start | bytes 1179656 | tf_op jit(solution)/shard_map/while/body/eval_jaxpr/ppermute | solution.py:19
  215.3 20.3 %collective-permute-start.4 = (bf16[3]{0:T(256)(128)(2,1)}, bf16[3]{0:T(256)(128)(2,1)S(1)}, u32[]{:S(2)}, u32[]{:S(2)}) collective-permute-start(bf16[3]{0:T(256)(128)(2,1)} %get-tuple-element.1047), channel_id=1, source_target_pairs={{0,15},{1,0},{2,1},{3,2},{4,3},{5,4},{6,5},{7,6},{8,7},{9,8},{10,9... | collective-permute-start | bytes 26 | tf_op jit(solution)/shard_map/while/body/eval_jaxpr/ppermute | solution.py:19
  221.1 18.2 %collective-permute-start = (bf16[3,256,256]{2,1,0:T(8,128)(2,1)}, bf16[3,256,256]{2,1,0:T(8,128)(2,1)S(1)}, u32[]{:S(2)}, u32[]{:S(2)}) collective-permute-start(bf16[3,256,256]{2,1,0:T(8,128)(2,1)} %get-tuple-element.1054), channel_id=1, source_target_pairs={{0,16},{16,32},{32,48},{48,64},{64,80},{80,96},{96,112},{112,128},... | collective-permute-start | bytes 1179656 | tf_op jit(solution)/shard_map/while/body/eval_jaxpr/ppermute | solution.py:19
  222.5 23.0 %collective-permute-start.5 = (bf16[3,256,256]{2,1,0:T(8,128)(2,1)}, bf16[3,256,256]{2,1,0:T(8,128)(2,1)}, u32[]{:S(2)}, u32[]{:S(2)}) collective-permute-start(bf16[3,256,256]{2,1,0:T(8,128)(2,1)} %get-tuple-element.1052), channel_id=1, source_target_pairs={{0,1},{1,2},{2,3},{3,4},{4,5},{5,6},{6,7},{7,8},{8,9},{9,10},{10,1... | collective-permute-start | bytes 1179656 | tf_op jit(solution)/shard_map/while/body/eval_jaxpr/ppermute | solution.py:19
  229.2 15.6 %collective-permute-start.7 = (bf16[3,256,256]{2,1,0:T(8,128)(2,1)}, bf16[3,256,256]{2,1,0:T(8,128)(2,1)S(1)}, u32[]{:S(2)}, u32[]{:S(2)}) collective-permute-start(bf16[3,256,256]{2,1,0:T(8,128)(2,1)} %get-tuple-element.1046), channel_id=1, source_target_pairs={{0,15},{1,0},{2,1},{3,2},{4,3},{5,4},{6,5},{7,6},{8,7},{9,8},{10,9... | collective-permute-start | bytes 1179656 | tf_op jit(solution)/shard_map/while/body/eval_jaxpr/ppermute | solution.py:19
  250.5 15.7 %collective-permute-start.1 = (bf16[3]{0:T(256)(128)(2,1)}, bf16[3]{0:T(256)(128)(2,1)S(1)}, u32[]{:S(2)}, u32[]{:S(2)}) collective-permute-start(bf16[3]{0:T(256)(128)(2,1)} %get-tuple-element.1049), channel_id=1, source_target_pairs={{0,240},{16,0},{32,16},{48,32},{64,48},{80,64},{96,80},{112,96},{1... | collective-permute-start | bytes 26 | tf_op jit(solution)/shard_map/while/body/eval_jaxpr/ppermute | solution.py:19
  252.0 20.8 %collective-permute-start.4 = (bf16[3]{0:T(256)(128)(2,1)}, bf16[3]{0:T(256)(128)(2,1)S(1)}, u32[]{:S(2)}, u32[]{:S(2)}) collective-permute-start(bf16[3]{0:T(256)(128)(2,1)} %get-tuple-element.1047), channel_id=1, source_target_pairs={{0,15},{1,0},{2,1},{3,2},{4,3},{5,4},{6,5},{7,6},{8,7},{9,8},{10,9... | collective-permute-start | bytes 26 | tf_op jit(solution)/shard_map/while/body/eval_jaxpr/ppermute | solution.py:19
  258.2 18.2 %collective-permute-start = (bf16[3,256,256]{2,1,0:T(8,128)(2,1)}, bf16[3,256,256]{2,1,0:T(8,128)(2,1)S(1)}, u32[]{:S(2)}, u32[]{:S(2)}) collective-permute-start(bf16[3,256,256]{2,1,0:T(8,128)(2,1)} %get-tuple-element.1054), channel_id=1, source_target_pairs={{0,16},{16,32},{32,48},{48,64},{64,80},{80,96},{96,112},{112,128},... | collective-permute-start | bytes 1179656 | tf_op jit(solution)/shard_map/while/body/eval_jaxpr/ppermute | solution.py:19
  259.6 23.0 %collective-permute-start.5 = (bf16[3,256,256]{2,1,0:T(8,128)(2,1)}, bf16[3,256,256]{2,1,0:T(8,128)(2,1)}, u32[]{:S(2)}, u32[]{:S(2)}) collective-permute-start(bf16[3,256,256]{2,1,0:T(8,128)(2,1)} %get-tuple-element.1052), channel_id=1, source_target_pairs={{0,1},{1,2},{2,3},{3,4},{4,5},{5,6},{6,7},{7,8},{8,9},{9,10},{10,1... | collective-permute-start | bytes 1179656 | tf_op jit(solution)/shard_map/while/body/eval_jaxpr/ppermute | solution.py:19
  266.3 15.6 %collective-permute-start.7 = (bf16[3,256,256]{2,1,0:T(8,128)(2,1)}, bf16[3,256,256]{2,1,0:T(8,128)(2,1)S(1)}, u32[]{:S(2)}, u32[]{:S(2)}) collective-permute-start(bf16[3,256,256]{2,1,0:T(8,128)(2,1)} %get-tuple-element.1046), channel_id=1, source_target_pairs={{0,15},{1,0},{2,1},{3,2},{4,3},{5,4},{6,5},{7,6},{8,7},{9,8},{10,9... | collective-permute-start | bytes 1179656 | tf_op jit(solution)/shard_map/while/body/eval_jaxpr/ppermute | solution.py:19
  287.6 15.7 %collective-permute-start.1 = (bf16[3]{0:T(256)(128)(2,1)}, bf16[3]{0:T(256)(128)(2,1)S(1)}, u32[]{:S(2)}, u32[]{:S(2)}) collective-permute-start(bf16[3]{0:T(256)(128)(2,1)} %get-tuple-element.1049), channel_id=1, source_target_pairs={{0,240},{16,0},{32,16},{48,32},{64,48},{80,64},{96,80},{112,96},{1... | collective-permute-start | bytes 26 | tf_op jit(solution)/shard_map/while/body/eval_jaxpr/ppermute | solution.py:19
  289.1 20.7 %collective-permute-start.4 = (bf16[3]{0:T(256)(128)(2,1)}, bf16[3]{0:T(256)(128)(2,1)S(1)}, u32[]{:S(2)}, u32[]{:S(2)}) collective-permute-start(bf16[3]{0:T(256)(128)(2,1)} %get-tuple-element.1047), channel_id=1, source_target_pairs={{0,15},{1,0},{2,1},{3,2},{4,3},{5,4},{6,5},{7,6},{8,7},{9,8},{10,9... | collective-permute-start | bytes 26 | tf_op jit(solution)/shard_map/while/body/eval_jaxpr/ppermute | solution.py:19
  295.3 18.2 %collective-permute-start = (bf16[3,256,256]{2,1,0:T(8,128)(2,1)}, bf16[3,256,256]{2,1,0:T(8,128)(2,1)S(1)}, u32[]{:S(2)}, u32[]{:S(2)}) collective-permute-start(bf16[3,256,256]{2,1,0:T(8,128)(2,1)} %get-tuple-element.1054), channel_id=1, source_target_pairs={{0,16},{16,32},{32,48},{48,64},{64,80},{80,96},{96,112},{112,128},... | collective-permute-start | bytes 1179656 | tf_op jit(solution)/shard_map/while/body/eval_jaxpr/ppermute | solution.py:19
  296.7 23.0 %collective-permute-start.5 = (bf16[3,256,256]{2,1,0:T(8,128)(2,1)}, bf16[3,256,256]{2,1,0:T(8,128)(2,1)}, u32[]{:S(2)}, u32[]{:S(2)}) collective-permute-start(bf16[3,256,256]{2,1,0:T(8,128)(2,1)} %get-tuple-element.1052), channel_id=1, source_target_pairs={{0,1},{1,2},{2,3},{3,4},{4,5},{5,6},{6,7},{7,8},{8,9},{9,10},{10,1... | collective-permute-start | bytes 1179656 | tf_op jit(solution)/shard_map/while/body/eval_jaxpr/ppermute | solution.py:19
  324.7 15.7 %collective-permute-start.1 = (bf16[3]{0:T(256)(128)(2,1)}, bf16[3]{0:T(256)(128)(2,1)S(1)}, u32[]{:S(2)}, u32[]{:S(2)}) collective-permute-start(bf16[3]{0:T(256)(128)(2,1)} %get-tuple-element.1049), channel_id=1, source_target_pairs={{0,240},{16,0},{32,16},{48,32},{64,48},{80,64},{96,80},{112,96},{1... | collective-permute-start | bytes 26 | tf_op jit(solution)/shard_map/while/body/eval_jaxpr/ppermute | solution.py:19
  326.2 20.7 %collective-permute-start.4 = (bf16[3]{0:T(256)(128)(2,1)}, bf16[3]{0:T(256)(128)(2,1)S(1)}, u32[]{:S(2)}, u32[]{:S(2)}) collective-permute-start(bf16[3]{0:T(256)(128)(2,1)} %get-tuple-element.1047), channel_id=1, source_target_pairs={{0,15},{1,0},{2,1},{3,2},{4,3},{5,4},{6,5},{7,6},{8,7},{9,8},{10,9... | collective-permute-start | bytes 26 | tf_op jit(solution)/shard_map/while/body/eval_jaxpr/ppermute | solution.py:19
  332.4 18.2 %collective-permute-start = (bf16[3,256,256]{2,1,0:T(8,128)(2,1)}, bf16[3,256,256]{2,1,0:T(8,128)(2,1)S(1)}, u32[]{:S(2)}, u32[]{:S(2)}) collective-permute-start(bf16[3,256,256]{2,1,0:T(8,128)(2,1)} %get-tuple-element.1054), channel_id=1, source_target_pairs={{0,16},{16,32},{32,48},{48,64},{64,80},{80,96},{96,112},{112,128},... | collective-permute-start | bytes 1179656 | tf_op jit(solution)/shard_map/while/body/eval_jaxpr/ppermute | solution.py:19
  333.8 23.0 %collective-permute-start.5 = (bf16[3,256,256]{2,1,0:T(8,128)(2,1)}, bf16[3,256,256]{2,1,0:T(8,128)(2,1)}, u32[]{:S(2)}, u32[]{:S(2)}) collective-permute-start(bf16[3,256,256]{2,1,0:T(8,128)(2,1)} %get-tuple-element.1052), channel_id=1, source_target_pairs={{0,1},{1,2},{2,3},{3,4},{4,5},{5,6},{6,7},{7,8},{8,9},{9,10},{10,1... | collective-permute-start | bytes 1179656 | tf_op jit(solution)/shard_map/while/body/eval_jaxpr/ppermute | solution.py:19
  386.9 19.7 %collective-permute-start.37 = (bf16[3,256,256]{1,2,0:T(8,128)(2,1)S(1)}, bf16[3,256,256]{1,2,0:T(8,128)(2,1)S(1)}, u32[]{:S(2)}, u32[]{:S(2)}) collective-permute-start(bf16[3,256,256]{1,2,0:T(8,128)(2,1)S(1)} %broadcast_select_fusion.7), channel_id=1, source_target_pairs={{0,14},{1,15},{2,0},{3,1},{4,2},{5,3},{6,4},{7,5},{8,6},{9,7},{10,... | collective-permute-start | bytes 1179656 | tf_op jit(solution)/shard_map/ppermute | solution.py:19
  416.2 20.9 %collective-permute-start.39 = (bf16[3,256,256]{1,2,0:T(8,128)(2,1)S(1)}, bf16[3,256,256]{1,2,0:T(8,128)(2,1)S(1)}, u32[]{:S(2)}, u32[]{:S(2)}) collective-permute-start(bf16[3,256,256]{1,2,0:T(8,128)(2,1)S(1)} %broadcast_select_fusion.11), channel_id=1, source_target_pairs={{0,8},{1,9},{2,10},{3,11},{4,12},{5,13},{6,14},{7,15},{8,0},{9,1},... | collective-permute-start | bytes 1179656 | tf_op jit(solution)/shard_map/ppermute | solution.py:19
  444.6 16.3 %collective-permute-start.8 = (bf16[3,256,256]{2,1,0:T(8,128)(2,1)}, bf16[3,256,256]{2,1,0:T(8,128)(2,1)S(1)}, u32[]{:S(2)}, u32[]{:S(2)}) collective-permute-start(bf16[3,256,256]{2,1,0:T(8,128)(2,1)} %get-tuple-element.1117), channel_id=1, source_target_pairs={{0,16},{16,32},{32,48},{48,64},{64,80},{80,96},{96,112},{112,128},... | collective-permute-start | bytes 1179656 | tf_op jit(solution)/shard_map/while/body/eval_jaxpr/ppermute | solution.py:19
  448.4 21.6 %collective-permute-start.13 = (bf16[3,256,256]{2,1,0:T(8,128)(2,1)}, bf16[3,256,256]{2,1,0:T(8,128)(2,1)}, u32[]{:S(2)}, u32[]{:S(2)}) collective-permute-start(bf16[3,256,256]{2,1,0:T(8,128)(2,1)} %get-tuple-element.1115), channel_id=1, source_target_pairs={{0,1},{1,2},{2,3},{3,4},{4,5},{5,6},{6,7},{7,8},{8,9},{9,10},{10,1... | collective-permute-start | bytes 1179656 | tf_op jit(solution)/shard_map/while/body/eval_jaxpr/ppermute | solution.py:19
  449.1 17.1 %collective-permute-start.14 = (bf16[3,256,256]{2,1,0:T(8,128)(2,1)}, bf16[3,256,256]{2,1,0:T(8,128)(2,1)S(1)}, u32[]{:S(2)}, u32[]{:S(2)}) collective-permute-start(bf16[3,256,256]{2,1,0:T(8,128)(2,1)} %get-tuple-element.1111), channel_id=1, source_target_pairs={{0,240},{16,0},{32,16},{48,32},{64,48},{80,64},{96,80},{112,96},{1... | collective-permute-start | bytes 1179656 | tf_op jit(solution)/shard_map/while/body/eval_jaxpr/ppermute | solution.py:19
  451.2 18.1 %collective-permute-start.15 = (bf16[3,256,256]{2,1,0:T(8,128)(2,1)}, bf16[3,256,256]{2,1,0:T(8,128)(2,1)S(1)}, u32[]{:S(2)}, u32[]{:S(2)}) collective-permute-start(bf16[3,256,256]{2,1,0:T(8,128)(2,1)} %get-tuple-element.1109), channel_id=1, source_target_pairs={{0,15},{1,0},{2,1},{3,2},{4,3},{5,4},{6,5},{7,6},{8,7},{9,8},{10,9... | collective-permute-start | bytes 1179656 | tf_op jit(solution)/shard_map/while/body/eval_jaxpr/ppermute | solution.py:19
  476.5 18.0 %collective-permute-start.12 = (bf16[3]{0:T(256)(128)(2,1)}, bf16[3]{0:T(256)(128)(2,1)S(1)}, u32[]{:S(2)}, u32[]{:S(2)}) collective-permute-start(bf16[3]{0:T(256)(128)(2,1)} %get-tuple-element.1110), channel_id=1, source_target_pairs={{0,15},{1,0},{2,1},{3,2},{4,3},{5,4},{6,5},{7,6},{8,7},{9,8},{10,9... | collective-permute-start | bytes 26 | tf_op jit(solution)/shard_map/while/body/eval_jaxpr/ppermute | solution.py:19
  481.4 16.7 %collective-permute-start.8 = (bf16[3,256,256]{2,1,0:T(8,128)(2,1)}, bf16[3,256,256]{2,1,0:T(8,128)(2,1)S(1)}, u32[]{:S(2)}, u32[]{:S(2)}) collective-permute-start(bf16[3,256,256]{2,1,0:T(8,128)(2,1)} %get-tuple-element.1117), channel_id=1, source_target_pairs={{0,16},{16,32},{32,48},{48,64},{64,80},{80,96},{96,112},{112,128},... | collective-permute-start | bytes 1179656 | tf_op jit(solution)/shard_map/while/body/eval_jaxpr/ppermute | solution.py:19
  482.8 23.6 %collective-permute-start.13 = (bf16[3,256,256]{2,1,0:T(8,128)(2,1)}, bf16[3,256,256]{2,1,0:T(8,128)(2,1)}, u32[]{:S(2)}, u32[]{:S(2)}) collective-permute-start(bf16[3,256,256]{2,1,0:T(8,128)(2,1)} %get-tuple-element.1115), channel_id=1, source_target_pairs={{0,1},{1,2},{2,3},{3,4},{4,5},{5,6},{6,7},{7,8},{8,9},{9,10},{10,1... | collective-permute-start | bytes 1179656 | tf_op jit(solution)/shard_map/while/body/eval_jaxpr/ppermute | solution.py:19
  486.3 16.3 %collective-permute-start.14 = (bf16[3,256,256]{2,1,0:T(8,128)(2,1)}, bf16[3,256,256]{2,1,0:T(8,128)(2,1)S(1)}, u32[]{:S(2)}, u32[]{:S(2)}) collective-permute-start(bf16[3,256,256]{2,1,0:T(8,128)(2,1)} %get-tuple-element.1111), channel_id=1, source_target_pairs={{0,240},{16,0},{32,16},{48,32},{64,48},{80,64},{96,80},{112,96},{1... | collective-permute-start | bytes 1179656 | tf_op jit(solution)/shard_map/while/body/eval_jaxpr/ppermute | solution.py:19
  488.4 17.4 %collective-permute-start.15 = (bf16[3,256,256]{2,1,0:T(8,128)(2,1)}, bf16[3,256,256]{2,1,0:T(8,128)(2,1)S(1)}, u32[]{:S(2)}, u32[]{:S(2)}) collective-permute-start(bf16[3,256,256]{2,1,0:T(8,128)(2,1)} %get-tuple-element.1109), channel_id=1, source_target_pairs={{0,15},{1,0},{2,1},{3,2},{4,3},{5,4},{6,5},{7,6},{8,7},{9,8},{10,9... | collective-permute-start | bytes 1179656 | tf_op jit(solution)/shard_map/while/body/eval_jaxpr/ppermute | solution.py:19
  512.9 18.2 %collective-permute-start.12 = (bf16[3]{0:T(256)(128)(2,1)}, bf16[3]{0:T(256)(128)(2,1)S(1)}, u32[]{:S(2)}, u32[]{:S(2)}) collective-permute-start(bf16[3]{0:T(256)(128)(2,1)} %get-tuple-element.1110), channel_id=1, source_target_pairs={{0,15},{1,0},{2,1},{3,2},{4,3},{5,4},{6,5},{7,6},{8,7},{9,8},{10,9... | collective-permute-start | bytes 26 | tf_op jit(solution)/shard_map/while/body/eval_jaxpr/ppermute | solution.py:19
  516.8 17.8 %collective-permute-start.8 = (bf16[3,256,256]{2,1,0:T(8,128)(2,1)}, bf16[3,256,256]{2,1,0:T(8,128)(2,1)S(1)}, u32[]{:S(2)}, u32[]{:S(2)}) collective-permute-start(bf16[3,256,256]{2,1,0:T(8,128)(2,1)} %get-tuple-element.1117), channel_id=1, source_target_pairs={{0,16},{16,32},{32,48},{48,64},{64,80},{80,96},{96,112},{112,128},... | collective-permute-start | bytes 1179656 | tf_op jit(solution)/shard_map/while/body/eval_jaxpr/ppermute | solution.py:19
  518.2 22.6 %collective-permute-start.13 = (bf16[3,256,256]{2,1,0:T(8,128)(2,1)}, bf16[3,256,256]{2,1,0:T(8,128)(2,1)}, u32[]{:S(2)}, u32[]{:S(2)}) collective-permute-start(bf16[3,256,256]{2,1,0:T(8,128)(2,1)} %get-tuple-element.1115), channel_id=1, source_target_pairs={{0,1},{1,2},{2,3},{3,4},{4,5},{5,6},{6,7},{7,8},{8,9},{9,10},{10,1... | collective-permute-start | bytes 1179656 | tf_op jit(solution)/shard_map/while/body/eval_jaxpr/ppermute | solution.py:19
  545.9 16.2 %collective-permute-start.9 = (bf16[3]{0:T(256)(128)(2,1)}, bf16[3]{0:T(256)(128)(2,1)S(1)}, u32[]{:S(2)}, u32[]{:S(2)}) collective-permute-start(bf16[3]{0:T(256)(128)(2,1)} %get-tuple-element.1112), channel_id=1, source_target_pairs={{0,240},{16,0},{32,16},{48,32},{64,48},{80,64},{96,80},{112,96},{1... | collective-permute-start | bytes 26 | tf_op jit(solution)/shard_map/while/body/eval_jaxpr/ppermute | solution.py:19
  547.3 20.9 %collective-permute-start.12 = (bf16[3]{0:T(256)(128)(2,1)}, bf16[3]{0:T(256)(128)(2,1)S(1)}, u32[]{:S(2)}, u32[]{:S(2)}) collective-permute-start(bf16[3]{0:T(256)(128)(2,1)} %get-tuple-element.1110), channel_id=1, source_target_pairs={{0,15},{1,0},{2,1},{3,2},{4,3},{5,4},{6,5},{7,6},{8,7},{9,8},{10,9... | collective-permute-start | bytes 26 | tf_op jit(solution)/shard_map/while/body/eval_jaxpr/ppermute | solution.py:19
  553.9 17.9 %collective-permute-start.8 = (bf16[3,256,256]{2,1,0:T(8,128)(2,1)}, bf16[3,256,256]{2,1,0:T(8,128)(2,1)S(1)}, u32[]{:S(2)}, u32[]{:S(2)}) collective-permute-start(bf16[3,256,256]{2,1,0:T(8,128)(2,1)} %get-tuple-element.1117), channel_id=1, source_target_pairs={{0,16},{16,32},{32,48},{48,64},{64,80},{80,96},{96,112},{112,128},... | collective-permute-start | bytes 1179656 | tf_op jit(solution)/shard_map/while/body/eval_jaxpr/ppermute | solution.py:19
  555.3 22.7 %collective-permute-start.13 = (bf16[3,256,256]{2,1,0:T(8,128)(2,1)}, bf16[3,256,256]{2,1,0:T(8,128)(2,1)}, u32[]{:S(2)}, u32[]{:S(2)}) collective-permute-start(bf16[3,256,256]{2,1,0:T(8,128)(2,1)} %get-tuple-element.1115), channel_id=1, source_target_pairs={{0,1},{1,2},{2,3},{3,4},{4,5},{5,6},{6,7},{7,8},{8,9},{9,10},{10,1... | collective-permute-start | bytes 1179656 | tf_op jit(solution)/shard_map/while/body/eval_jaxpr/ppermute | solution.py:19
  583.0 16.1 %collective-permute-start.9 = (bf16[3]{0:T(256)(128)(2,1)}, bf16[3]{0:T(256)(128)(2,1)S(1)}, u32[]{:S(2)}, u32[]{:S(2)}) collective-permute-start(bf16[3]{0:T(256)(128)(2,1)} %get-tuple-element.1112), channel_id=1, source_target_pairs={{0,240},{16,0},{32,16},{48,32},{64,48},{80,64},{96,80},{112,96},{1... | collective-permute-start | bytes 26 | tf_op jit(solution)/shard_map/while/body/eval_jaxpr/ppermute | solution.py:19
  584.4 20.9 %collective-permute-start.12 = (bf16[3]{0:T(256)(128)(2,1)}, bf16[3]{0:T(256)(128)(2,1)S(1)}, u32[]{:S(2)}, u32[]{:S(2)}) collective-permute-start(bf16[3]{0:T(256)(128)(2,1)} %get-tuple-element.1110), channel_id=1, source_target_pairs={{0,15},{1,0},{2,1},{3,2},{4,3},{5,4},{6,5},{7,6},{8,7},{9,8},{10,9... | collective-permute-start | bytes 26 | tf_op jit(solution)/shard_map/while/body/eval_jaxpr/ppermute | solution.py:19
  591.0 17.9 %collective-permute-start.8 = (bf16[3,256,256]{2,1,0:T(8,128)(2,1)}, bf16[3,256,256]{2,1,0:T(8,128)(2,1)S(1)}, u32[]{:S(2)}, u32[]{:S(2)}) collective-permute-start(bf16[3,256,256]{2,1,0:T(8,128)(2,1)} %get-tuple-element.1117), channel_id=1, source_target_pairs={{0,16},{16,32},{32,48},{48,64},{64,80},{80,96},{96,112},{112,128},... | collective-permute-start | bytes 1179656 | tf_op jit(solution)/shard_map/while/body/eval_jaxpr/ppermute | solution.py:19
  592.4 22.7 %collective-permute-start.13 = (bf16[3,256,256]{2,1,0:T(8,128)(2,1)}, bf16[3,256,256]{2,1,0:T(8,128)(2,1)}, u32[]{:S(2)}, u32[]{:S(2)}) collective-permute-start(bf16[3,256,256]{2,1,0:T(8,128)(2,1)} %get-tuple-element.1115), channel_id=1, source_target_pairs={{0,1},{1,2},{2,3},{3,4},{4,5},{5,6},{6,7},{7,8},{8,9},{9,10},{10,1... | collective-permute-start | bytes 1179656 | tf_op jit(solution)/shard_map/while/body/eval_jaxpr/ppermute | solution.py:19
  620.0 16.1 %collective-permute-start.9 = (bf16[3]{0:T(256)(128)(2,1)}, bf16[3]{0:T(256)(128)(2,1)S(1)}, u32[]{:S(2)}, u32[]{:S(2)}) collective-permute-start(bf16[3]{0:T(256)(128)(2,1)} %get-tuple-element.1112), channel_id=1, source_target_pairs={{0,240},{16,0},{32,16},{48,32},{64,48},{80,64},{96,80},{112,96},{1... | collective-permute-start | bytes 26 | tf_op jit(solution)/shard_map/while/body/eval_jaxpr/ppermute | solution.py:19
  621.5 20.9 %collective-permute-start.12 = (bf16[3]{0:T(256)(128)(2,1)}, bf16[3]{0:T(256)(128)(2,1)S(1)}, u32[]{:S(2)}, u32[]{:S(2)}) collective-permute-start(bf16[3]{0:T(256)(128)(2,1)} %get-tuple-element.1110), channel_id=1, source_target_pairs={{0,15},{1,0},{2,1},{3,2},{4,3},{5,4},{6,5},{7,6},{8,7},{9,8},{10,9... | collective-permute-start | bytes 26 | tf_op jit(solution)/shard_map/while/body/eval_jaxpr/ppermute | solution.py:19
  628.0 17.9 %collective-permute-start.8 = (bf16[3,256,256]{2,1,0:T(8,128)(2,1)}, bf16[3,256,256]{2,1,0:T(8,128)(2,1)S(1)}, u32[]{:S(2)}, u32[]{:S(2)}) collective-permute-start(bf16[3,256,256]{2,1,0:T(8,128)(2,1)} %get-tuple-element.1117), channel_id=1, source_target_pairs={{0,16},{16,32},{32,48},{48,64},{64,80},{80,96},{96,112},{112,128},... | collective-permute-start | bytes 1179656 | tf_op jit(solution)/shard_map/while/body/eval_jaxpr/ppermute | solution.py:19
  629.4 22.7 %collective-permute-start.13 = (bf16[3,256,256]{2,1,0:T(8,128)(2,1)}, bf16[3,256,256]{2,1,0:T(8,128)(2,1)}, u32[]{:S(2)}, u32[]{:S(2)}) collective-permute-start(bf16[3,256,256]{2,1,0:T(8,128)(2,1)} %get-tuple-element.1115), channel_id=1, source_target_pairs={{0,1},{1,2},{2,3},{3,4},{4,5},{5,6},{6,7},{7,8},{8,9},{9,10},{10,1... | collective-permute-start | bytes 1179656 | tf_op jit(solution)/shard_map/while/body/eval_jaxpr/ppermute | solution.py:19
  657.1 16.1 %collective-permute-start.9 = (bf16[3]{0:T(256)(128)(2,1)}, bf16[3]{0:T(256)(128)(2,1)S(1)}, u32[]{:S(2)}, u32[]{:S(2)}) collective-permute-start(bf16[3]{0:T(256)(128)(2,1)} %get-tuple-element.1112), channel_id=1, source_target_pairs={{0,240},{16,0},{32,16},{48,32},{64,48},{80,64},{96,80},{112,96},{1... | collective-permute-start | bytes 26 | tf_op jit(solution)/shard_map/while/body/eval_jaxpr/ppermute | solution.py:19
  658.6 20.9 %collective-permute-start.12 = (bf16[3]{0:T(256)(128)(2,1)}, bf16[3]{0:T(256)(128)(2,1)S(1)}, u32[]{:S(2)}, u32[]{:S(2)}) collective-permute-start(bf16[3]{0:T(256)(128)(2,1)} %get-tuple-element.1110), channel_id=1, source_target_pairs={{0,15},{1,0},{2,1},{3,2},{4,3},{5,4},{6,5},{7,6},{8,7},{9,8},{10,9... | collective-permute-start | bytes 26 | tf_op jit(solution)/shard_map/while/body/eval_jaxpr/ppermute | solution.py:19
  665.1 17.9 %collective-permute-start.8 = (bf16[3,256,256]{2,1,0:T(8,128)(2,1)}, bf16[3,256,256]{2,1,0:T(8,128)(2,1)S(1)}, u32[]{:S(2)}, u32[]{:S(2)}) collective-permute-start(bf16[3,256,256]{2,1,0:T(8,128)(2,1)} %get-tuple-element.1117), channel_id=1, source_target_pairs={{0,16},{16,32},{32,48},{48,64},{64,80},{80,96},{96,112},{112,128},... | collective-permute-start | bytes 1179656 | tf_op jit(solution)/shard_map/while/body/eval_jaxpr/ppermute | solution.py:19
  666.5 22.7 %collective-permute-start.13 = (bf16[3,256,256]{2,1,0:T(8,128)(2,1)}, bf16[3,256,256]{2,1,0:T(8,128)(2,1)}, u32[]{:S(2)}, u32[]{:S(2)}) collective-permute-start(bf16[3,256,256]{2,1,0:T(8,128)(2,1)} %get-tuple-element.1115), channel_id=1, source_target_pairs={{0,1},{1,2},{2,3},{3,4},{4,5},{5,6},{6,7},{7,8},{8,9},{9,10},{10,1... | collective-permute-start | bytes 1179656 | tf_op jit(solution)/shard_map/while/body/eval_jaxpr/ppermute | solution.py:19
  (144 other events, 1086.1 us)
where the time goes:
time: 725 us; the launch traced here: 713 us
  starting transfers between devices  341 us (47%)
  local copies, waits for them, and re-layouts  176 us (24%)
  waiting for transfers between devices  100 us (14%)
  other arithmetic  56.4 us (8%)
  matrix products  37 us (5%)
    ppermute x140, starting transfers between devices, shifted(): lax.ppermute(shard, axis, [(i, (i + by) % length) for i in range(length)])  341 us
    ppermute x140, waiting for transfers between devices, shifted(): lax.ppermute(shard, axis, [(i, (i + by) % length) for i in range(length)])  100 us
    while x224, local copies, waits for them, and re-layouts  98.9 us
    dot_general x32, matrix products, contribution(): jnp.einsum('ixy,siyz->sxz', left_tiles, picked, preferred_element_type=jn...  36 us
    reshape x30, local copies, waits for them, and re-layouts, contribution(): picked.reshape(slot_count, slot_count, side, side)  33.6 us
    gather x31, local copies, waits for them, and re-layouts, contribution(): jnp.take(right_tiles, index.reshape(slot_count * slot_count), axis=0)  19.3 us
    unnamed x36, local copies, waits for them, and re-layouts  18.1 us
  transfers between devices with their start and end apart: 140, of which 31 were waited for; matrix products, arithmetic and copies ran while one was open for 26% of the time, Pallas kernels for 0%

commit v1 on v0

v1 whole, which is shorter than its diff:
```python
import functools

import jax
import jax.numpy as jnp
from jax import lax
from jax.experimental import pallas as pl
from jax.experimental.pallas import tpu as pltpu
from jax.sharding import PartitionSpec as P

MESH = pl.DeviceIdType.MESH
BS = 256
HALF = BS // 2
SENDS = 200
ZERO = 48


def device(z, xlo, xhi, y, core):
    return (z * 2 + xlo, (xhi * 4 + y) * 2 + core)


def kernel(
    tiles, stack, mask, out,
    colbuf, rowbuf, sqbuf, stage, acc, near_table, far_table,
    send_sem, col_sem, row_sem, sq_sem,
):
    r = lax.axis_index("row")
    c = lax.axis_index("col")
    z, xlo = r // 2, r % 2
    xhi, y, core = c // 8, (c // 2) % 4, c % 2
    sign = 1 - 2 * core
    xlo2, xhi2, core2 = 1 - xlo, 1 - xhi, 1 - core

    def zat(steps):
        return (z + sign * steps + 8) % 8

    def yat(steps):
        return (y + steps + 4) % 4

    to_za = device(zat(1), xlo, xhi, y, core)
    to_zb = device(zat(-1), xlo, xhi, y, core)
    to_yc = device(z, xlo, xhi, yat(1), core)
    to_yd = device(z, xlo, xhi, yat(-1), core)
    to_xlo = device(z, xlo2, xhi, y, core)
    to_xhi = device(z, xlo, xhi2, y, core)
    to_core = device(z, xlo, xhi, y, core2)
    peers = (to_za, to_zb, to_yc, to_yd, to_xlo, to_xhi, to_core)

    barrier = pltpu.get_barrier_semaphore()
    for peer in peers:
        pl.semaphore_signal(barrier, inc=1, device_id=peer, device_id_type=MESH)

    ids = [stack[0, 0, s] for s in range(3)]
    live = [mask[4 * r + ids[s] // 4, 4 * c + ids[s] % 4] > 0 for s in range(3)]
    rank = []
    for s in range(3):
        below = jnp.int32(0)
        for t in range(3):
            if t != s:
                below = below + jnp.where(live[t] & (ids[t] < ids[s]), 1, 0)
        rank.append(jnp.where(live[s], below, 3))
    own_ids = []
    for q in range(3):
        place = jnp.int32(0)
        own_id = jnp.int32(-1)
        for s in range(3):
            place = jnp.where(rank[s] == q, s, place)
            own_id = jnp.where(rank[s] == q, ids[s], own_id)
        own_ids.append(own_id)
        tile = tiles[place]
        colbuf[3 * r + q] = tile
        rowbuf[3 * c + q] = tile
    zero = jnp.zeros((BS, BS), jnp.bfloat16)
    stage[3] = zero
    colbuf[ZERO] = zero
    acc[...] = jnp.zeros_like(acc)

    pl.semaphore_wait(barrier, len(peers))

    started = []

    def piece(buf, place, part):
        if part is None:
            return buf.at[place]
        return buf.at[place, pl.ds(part * HALF, HALF)]

    def remote(buf, sems, region, unit, target):
        slot, part = {0: (0, None), 1: (1, None), 2: (2, None), 3: (2, 0), 4: (2, 1)}[unit]
        ref = piece(buf, 3 * region + slot, part)
        sem = sems.at[4 * region + {0: 0, 1: 1, 2: 2, 3: 2, 4: 3}[unit]]
        return pltpu.make_async_remote_copy(
            src_ref=ref, dst_ref=ref, send_sem=send_sem.at[len(started)], recv_sem=sem,
            device_id=target, device_id_type=MESH,
        )

    def send(buf, sems, region, unit, *targets):
        for target in targets:
            copy = remote(buf, sems, region, unit, target)
            copy.start()
            started.append(copy)

    def landed(buf, sems, region, *units):
        for unit in units:
            remote(buf, sems, region, unit, to_core).wait_recv()

    col = (colbuf, col_sem)

    def own_row(steps):
        return 2 * zat(steps) + xlo

    def par_row(steps):
        return 2 * zat(steps) + xlo2

    def cat(by, steps, own_core=True, own_xhi=True):
        return ((xhi if own_xhi else xhi2) * 4 + yat(steps)) * 2 + (core if own_core else core2)

    class Row:
        def __init__(self, buf, sems, x_first, y_first):
            self.b = (buf, sems)
            self.xf, self.yf = x_first, y_first

        def begin(self):
            me = cat("y", 0)
            for s in self.xf:
                send(*self.b, me, s, to_xhi)
            for s in self.yf + self.xf:
                send(*self.b, me, s, to_yc, to_yd)
            for s in self.yf:
                send(*self.b, me, s, to_xhi)
            for s in range(3):
                send(*self.b, me, s, to_core)

        def x_hop(self):
            par = cat("y", 0, own_xhi=False)
            for s in self.xf:
                landed(*self.b, par, s)
                send(*self.b, par, s, to_yc, to_yd, to_core)

        def y_near_first(self):
            for s in self.yf:
                for way, target, unit in ((-1, to_yc, 3), (1, to_yd, 4)):
                    region = cat("y", way)
                    landed(*self.b, region, s)
                    send(*self.b, region, unit, target)
                    send(*self.b, region, s, to_xhi, to_core)

        def y_near_own(self):
            for s in self.xf:
                landed(*self.b, cat("y", -1), s)
                send(*self.b, cat("y", -1), s, to_yc, to_core)
                landed(*self.b, cat("y", 1), s)
                send(*self.b, cat("y", 1), s, to_core)

        def y_near_par(self):
            for s in self.xf:
                landed(*self.b, cat("y", 1, own_xhi=False), s)
                send(*self.b, cat("y", 1, own_xhi=False), s, to_yd, to_core)
                landed(*self.b, cat("y", -1, own_xhi=False), s)
                send(*self.b, cat("y", -1, own_xhi=False), s, to_core)

        def x_late(self, *steps):
            for step in steps:
                for s in self.yf:
                    region = cat("y", step, own_xhi=False)
                    landed(*self.b, region, s)
                    send(*self.b, region, s, to_core)

        def y_far_first(self):
            for s in self.yf:
                region = cat("y", 2)
                for unit in (3, 4):
                    landed(*self.b, region, unit)
                    send(*self.b, region, unit, to_xhi)
                send(*self.b, region, s, to_core)

        def y_far(self):
            for s in self.xf:
                landed(*self.b, cat("y", 2), s)
                send(*self.b, cat("y", 2), s, to_core)
                landed(*self.b, cat("y", 2, own_xhi=False), s)
                send(*self.b, cat("y", 2, own_xhi=False), s, to_core)

        def x_last(self):
            for s in self.yf:
                region = cat("y", 2, own_xhi=False)
                landed(*self.b, region, 3, 4)
                send(*self.b, region, s, to_core)

        def sibling(self, steps, own_xhi=True):
            landed(*self.b, cat("y", steps, own_core=False, own_xhi=own_xhi), 0, 1, 2)

    def z_near(steps, *units, last=False):
        for unit in units:
            own = unit in (0, 1, 2)
            slot = unit if own else unit - 3
            for way in (1, -1):
                region = own_row(-way * steps) if own else par_row(-way * steps)
                target = to_za if way == 1 else to_zb
                landed(*col, region, slot)
                if not last:
                    send(*col, region, slot, target)
                elif slot == 2:
                    send(*col, region, 3 if way == 1 else 4, target)
                elif own == (way == 1):
                    send(*col, region, slot, target)
                if slot == 2:
                    send(*col, region, 2, to_xlo)

    row = Row(rowbuf, row_sem, [0, 1, 2], [])
    sq = Row(sqbuf, sq_sem, [0, 1], [2])

    send(*col, r, 0, to_xlo)
    send(*col, r, 1, to_xlo)
    for s in (2, 0, 1):
        send(*col, r, s, to_za, to_zb)
    send(*col, r, 2, to_xlo)
    row.begin()

    def table(p, carry):
        left = [jnp.int32(-1)] * 3
        count = jnp.int32(0)
        for b in range(16):
            here = mask[4 * r + b // 4, 4 * p + b % 4] > 0
            for l in range(3):
                left[l] = jnp.where(here & (count == l), b, left[l])
            count = count + jnp.where(here, 1, 0)
        word = jnp.int32(0)
        count = jnp.int32(0)
        places = []
        for b in range(16):
            here = mask[4 * p + b // 4, 4 * c + b % 4] > 0
            places.append(jnp.where(here, count, 3))
            count = count + jnp.where(here, 1, 0)
        for q in range(3):
            own = own_ids[q]
            column = [jnp.int32(3)] * 4
            for kk in range(4):
                for b in range(4):
                    column[kk] = jnp.where(own % 4 == b, places[4 * kk + b], column[kk])
            for l in range(3):
                found = jnp.int32(3)
                for kk in range(4):
                    found = jnp.where(left[l] % 4 == kk, column[kk], found)
                good = (own >= 0) & (left[l] >= 0) & (left[l] // 4 == own // 4)
                found = jnp.where(good, found, 3)
                near_table[p, 3 * q + l] = found
                far_table[p, 3 * q + l] = jnp.where(found < 3, 3 * p + found, ZERO)
        return carry

    lax.fori_loop(0, 16, table, 0)

    def near_step(p):
        for s in range(3):
            stage[s] = colbuf[3 * p + s]
        for q in range(3):
            total = acc[q]
            for l in range(3):
                total = total + jnp.dot(
                    rowbuf[3 * p + l], stage[near_table[p, 3 * q + l]],
                    preferred_element_type=jnp.float32,
                )
            acc[q] = total

    def far_step(p):
        for q in range(3):
            total = acc[q]
            for l in range(3):
                total = total + jnp.dot(
                    sqbuf[3 * p + l], colbuf[far_table[p, 3 * q + l]],
                    preferred_element_type=jnp.float32,
                )
            acc[q] = total

    def each(count, where, step):
        def body(i, carry):
            step(where(i))
            return carry

        lax.fori_loop(0, count, body, 0)

    def ring_region(steps):
        return lambda i: 2 * zat((1 - 2 * (i // 2)) * steps) + i % 2

    z_near(1, 2)
    landed(*col, par_row(0), 0)
    send(*col, par_row(0), 0, to_za, to_zb)
    landed(*col, par_row(0), 1)
    send(*col, par_row(0), 1, to_za, to_zb)
    z_near(1, 0, 1)
    row.y_near_own()
    row.x_hop()
    z_near(1, 3, 4)
    row.y_near_par()
    z_near(2, 2, 0, 1)
    row.y_far()
    z_near(2, 3, 4)
    for steps in (0, 1, -1, 2):
        row.sibling(steps)
        row.sibling(steps, own_xhi=False)
    landed(*col, par_row(0), 2)
    each(2, lambda i: 2 * z + i, near_step)
    z_near(3, 2, last=True)
    for way in (1, -1):
        landed(*col, par_row(way), 2)
    each(4, ring_region(1), near_step)
    z_near(3, 0, last=True)
    for way in (2, -2):
        landed(*col, par_row(way), 2)
    each(4, ring_region(2), near_step)
    z_near(3, 1, 3, 4, last=True)
    landed(*col, own_row(4), 3)
    send(*col, own_row(4), 3, to_xlo)
    landed(*col, own_row(4), 4)
    send(*col, own_row(4), 4, to_xlo)
    for way in (3, -3):
        landed(*col, par_row(way), 2)
    each(4, ring_region(3), near_step)
    landed(*col, own_row(4), 0, 1)
    landed(*col, par_row(4), 3, 4, 0, 1)
    each(2, lambda i: 2 * zat(4) + i, near_step)

    for q in range(3):
        sqbuf[3 * c + q] = acc[q].astype(jnp.bfloat16)
    sq.begin()
    acc[...] = jnp.zeros_like(acc)

    def own_chip(step):
        return lambda i: (xhi * 4 + yat(step)) * 2 + i

    sq.sibling(0)
    each(2, lambda i: (xhi * 4 + y) * 2 + i, far_step)
    sq.y_near_first()
    sq.x_hop()
    sq.y_near_own()
    sq.x_late(0)
    sq.sibling(0, own_xhi=False)
    each(2, lambda i: (xhi2 * 4 + y) * 2 + i, far_step)
    sq.sibling(1)
    sq.sibling(-1)
    each(4, lambda i: (xhi * 4 + yat(1 - 2 * (i // 2))) * 2 + i % 2, far_step)
    sq.y_near_par()
    sq.x_late(1, -1)
    sq.y_far_first()
    sq.sibling(1, own_xhi=False)
    sq.sibling(-1, own_xhi=False)
    each(4, lambda i: (xhi2 * 4 + yat(1 - 2 * (i // 2))) * 2 + i % 2, far_step)
    sq.y_far()
    sq.x_last()
    each(2, lambda i: ((xhi + i) % 2 * 4 + yat(2)) * 2 + core, far_step)
    sq.sibling(2)
    sq.sibling(2, own_xhi=False)
    each(2, lambda i: ((xhi + i) % 2 * 4 + yat(2)) * 2 + core2, far_step)

    stage[3] = zero
    for q in range(3):
        stage[q] = sqbuf[3 * c + q]
    for s in range(3):
        place = jnp.minimum(rank[s], 2)
        value = 3.0 * stage[place].astype(jnp.float32) - 2.0 * acc[place]
        out[s] = jnp.where(live[s], value, 0.0).astype(jnp.bfloat16)

    for copy in started:
        copy.wait_send()


def local(tiles, stack, mask):
    vmem = pl.BlockSpec(memory_space=pltpu.VMEM)
    smem = pl.BlockSpec(memory_space=pltpu.SMEM)
    result = pl.pallas_call(
        kernel,
        out_shape=jax.ShapeDtypeStruct((3, BS, BS), jnp.bfloat16),
        in_specs=[vmem, smem, smem],
        out_specs=vmem,
        scratch_shapes=[
            pltpu.VMEM((49, BS, BS), jnp.bfloat16),
            pltpu.VMEM((48, BS, BS), jnp.bfloat16),
            pltpu.VMEM((48, BS, BS), jnp.bfloat16),
            pltpu.VMEM((4, BS, BS), jnp.bfloat16),
            pltpu.VMEM((3, BS, BS), jnp.float32),
            pltpu.SMEM((16, 9), jnp.int32),
            pltpu.SMEM((16, 9), jnp.int32),
            pltpu.SemaphoreType.DMA((SENDS,)),
            pltpu.SemaphoreType.DMA((64,)),
            pltpu.SemaphoreType.DMA((64,)),
            pltpu.SemaphoreType.DMA((64,)),
        ],
        compiler_params=pltpu.CompilerParams(
            collective_id=0, has_side_effects=True, vmem_limit_bytes=40 * 1024 * 1024
        ),
        name="purify",
    )(tiles[0, 0], stack, mask)
    return result[None, None]


def solution(mesh):
    placed = (P("row", "col", None, None, None), P("row", "col", None), P())
    return jax.shard_map(
        local,
        mesh=mesh,
        in_specs=placed,
        out_specs=P("row", "col", None, None, None),
        check_vma=False,
    )
```

time: 725 us -> 95.5 us (0.13); the launches traced: 713 us -> 95.3 us
  starting transfers between devices: 341 us -> 0 us
  local copies, waits for them, and re-layouts: 176 us -> 3.16 us
  waiting for transfers between devices: 100 us -> 0 us
  Pallas kernels: 0 us -> 92.2 us
  other arithmetic: 56.4 us -> 0 us
  matrix products: 37 us -> 0 us
    ppermute x140 -> x0, starting transfers between devices: 341 us -> none  [shifted(): lax.ppermute(shard, axis, [(i, (i + by) % length) for i in range(length)])]
    while x227 -> x0, local copies, waits for them, and re-layouts: 102 us -> none
    ppermute x140 -> x0, waiting for transfers between devices: 100 us -> none  [shifted(): lax.ppermute(shard, axis, [(i, (i + by) % length) for i in range(length)])]
    pallas_call x0 -> x1, Pallas kernels: none -> 92.2 us  [local(): pl.pallas_call(kernel, out_shape=jax.ShapeDtypeStruct((3, BS, BS), jnp.bf...]
    dot_general x33 -> x0, matrix products: 37 us -> none  [the longest x32 36 us: contribution(): jnp.einsum('ixy,siyz->sxz', left_tiles, picked, preferred_element_type=jn...]
    reshape x61 -> x0, local copies, waits for them, and re-layouts: 36.1 us -> none  [the longest x30 33.6 us: contribution(): picked.reshape(slot_count, slot_count, side, side)]
    gather x31 -> x0, local copies, waits for them, and re-layouts: 19.3 us -> none  [contribution(): jnp.take(right_tiles, index.reshape(slot_count * slot_count), axis=0)]
    select_n x124 -> x0, other arithmetic: 18.3 us -> none  [the longest x15 10.5 us: contribution(): own_row = own_ids // block_cols]
  transfers between devices with their start and end apart: 140 -> 0, of which waited for: 31 -> 0; matrix products, arithmetic and copies ran while one was open for 26% -> 0% of each run, Pallas kernels for 0% -> 0%
where the time goes in v1:
time: 95.5 us; the launch traced here: 95.3 us
  Pallas kernels  92.2 us (97%)
  local copies, waits for them, and re-layouts  3.16 us (3%)
    pallas_call x1, Pallas kernels, local(): pl.pallas_call(kernel, out_shape=jax.ShapeDtypeStruct((3, BS, BS), jnp.bf...  92.2 us
    unnamed x7, local copies, waits for them, and re-layouts  3.16 us

profile of v1, /device:TPU:1, one launch (start us, length us, event | category | flops | bytes accessed | tf_op | source)
XLA Modules:
  0.0 95.3 jit_solution(1341412929460717081)
XLA Ops:
  0.0 0.0 copy-start.2
  0.0 0.7 copy-done.2
  0.7 0.0 copy-start
  0.7 1.0 %copy-done = bf16[1,1,3,256,256]{4,3,2,1,0:T(8,128)(2,1)S(1)} copy-done((bf16[1,1,3,256,256]{4,3,2,1,0:T(8,128)(2,1)S(1)}, bf16[1,1,3,256,256]{4,3,2,1,0:T(8,128)(2,1)}, u32[]{:S(2)}) %copy-start) | copy-done | bytes 393240
  1.7 0.0 copy-start.1
  1.7 0.8 copy-done.1
  2.4 92.2 %purify.1 = bf16[3,256,256]{2,1,0:T(8,128)(2,1)S(1)} custom-call(bf16[3,256,256]{2,1,0:T(8,128)(2,1)S(1)} %bitcast.3, s32[1,1,3]{2,1,0:T(1,128)S(1)} %copy-done.2, s32[64,64]{1,0:T(8,128)S(1)} %copy-done.1), custom_call_target="tpu_custom_call" | custom-call | tf_op jit(solution)/shard_map/purify/pallas_call | solution.py:368
  94.6 0.7 copy.5
Async XLA Ops:
  0.0 0.7 copy-start.2
  0.7 1.0 %copy-start = (bf16[1,1,3,256,256]{4,3,2,1,0:T(8,128)(2,1)S(1)}, bf16[1,1,3,256,256]{4,3,2,1,0:T(8,128)(2,1)}, u32[]{:S(2)}) copy-start(bf16[1,1,3,256,256]{4,3,2,1,0:T(8,128)(2,1)} %param.3) | copy-start | bytes 1179652
  1.7 0.8 copy-start.1

commit v2 on v1

v2 whole, which is shorter than its diff:
```python
import jax
import jax.numpy as jnp
from jax import lax
from jax.experimental import pallas as pl
from jax.experimental.pallas import tpu as pltpu
from jax.sharding import PartitionSpec as P

MESH = pl.DeviceIdType.MESH
BS = 256
LANES = 128
REGION = 3 * BS
NAMES = 72
X_ROWS = 448
Y_ROWS = 320


def device(z, xlo, xhi, y, core):
    return (z * 2 + xlo, (xhi * 4 + y) * 2 + core)


def kernel(
    tiles_in, stack_in, mask_in, out,
    tiles, stack, mask, colbuf, rowbuf, sqbuf, stage, far_stage, near_acc, acc, meets,
    in_sem, send_sem, recv_sem,
):
    r = lax.axis_index("row")
    c = lax.axis_index("col")
    z, xlo = r // 2, r % 2
    xhi, y, core = c // 8, (c // 2) % 4, c % 2
    sign = 1 - 2 * core
    xlo2, xhi2, core2 = 1 - xlo, 1 - xhi, 1 - core

    def zat(steps):
        return (z + sign * steps + 8) % 8

    def yat(steps):
        return (y + steps + 4) % 4

    to_za = device(zat(1), xlo, xhi, y, core)
    to_zb = device(zat(-1), xlo, xhi, y, core)
    to_yc = device(z, xlo, xhi, yat(1), core)
    to_yd = device(z, xlo, xhi, yat(-1), core)
    to_xlo = device(z, xlo2, xhi, y, core)
    to_xhi = device(z, xlo, xhi2, y, core)
    to_core = device(z, xlo, xhi, y, core2)
    peers = (to_za, to_zb, to_yc, to_yd, to_xlo, to_xhi, to_core)

    barrier = pltpu.get_barrier_semaphore()
    for peer in peers:
        pl.semaphore_signal(barrier, inc=1, device_id=peer, device_id_type=MESH)
    loads = [
        pltpu.make_async_copy(mask_in, mask, in_sem.at[0]),
        pltpu.make_async_copy(stack_in, stack, in_sem.at[1]),
        pltpu.make_async_copy(tiles_in, tiles.at[pl.ds(0, 3)], in_sem.at[2]),
    ]
    for load in loads:
        load.start()
    zero = jnp.zeros((BS, BS), jnp.bfloat16)
    stage[3] = zero[:, :LANES]
    for half in range(2):
        far_stage[half, 3] = zero[:LANES]
    near_acc[...] = jnp.zeros_like(near_acc)
    acc[...] = jnp.zeros_like(acc)
    for load in loads:
        load.wait()

    def rows_of(place, first=0, count=BS):
        return pl.ds(pl.multiple_of(place * BS + first, 16), count)

    ids = [stack[0, 0, s] for s in range(3)]
    live = [mask[4 * r + ids[s] // 4, 4 * c + ids[s] % 4] > 0 for s in range(3)]
    rank = []
    for s in range(3):
        below = jnp.int32(0)
        for t in range(3):
            if t != s:
                below = below + jnp.where(live[t] & (ids[t] < ids[s]), 1, 0)
        rank.append(jnp.where(live[s], below, 3))
    own_ids = []
    for q in range(3):
        place = jnp.int32(0)
        own_id = jnp.int32(-1)
        for s in range(3):
            place = jnp.where(rank[s] == q, s, place)
            own_id = jnp.where(rank[s] == q, ids[s], own_id)
        own_ids.append(own_id)
        tile = tiles[place]
        colbuf[rows_of(3 * r + q)] = tile
        rowbuf[rows_of(3 * c + q)] = tile

    pl.semaphore_wait(barrier, len(peers))

    recv_names, panels = {}, {}

    class Panel:
        def __init__(self, buf, half, units):
            self.buf, self.half, self.units = buf, half, units
            self.tag = len(panels)
            panels[self.tag] = self
            self.sent = 0

        def block(self, rows):
            if self.half is None:
                return self.buf.at[rows]
            return self.buf.at[rows, pl.ds(self.half * LANES, LANES)]

        def copy(self, ref, name, target):
            index = recv_names.setdefault((self.tag, *name), len(recv_names))
            return pltpu.make_async_remote_copy(
                src_ref=ref, dst_ref=ref, send_sem=send_sem.at[self.tag],
                recv_sem=recv_sem.at[index], device_id=target, device_id_type=MESH,
            )

        def send(self, region, unit, name, *targets):
            first, count = self.units[unit]
            ref = self.block(rows_of(3 * region, first, count))
            self.last = name
            for target in targets:
                self.copy(ref, name, target).start()
                self.sent += count

        def landed(self, name, count):
            self.copy(self.block(pl.ds(0, count)), name, to_core).wait_recv()

        def drain(self):
            self.copy(self.block(pl.ds(0, self.sent)), self.last, to_core).wait_send()

    def own_row(steps):
        return 2 * zat(steps) + xlo

    def par_row(steps):
        return 2 * zat(steps) + xlo2

    z_rows = REGION - X_ROWS
    col_units = {
        "x": (0, X_ROWS),
        "z": (X_ROWS, z_rows),
        "z0": (X_ROWS, z_rows // 2),
        "z1": (X_ROWS + z_rows // 2, z_rows // 2),
    }

    class Column(Panel):
        def __init__(self, half, groups):
            super().__init__(colbuf, half, col_units)
            self.groups = groups

        def cross(self, region, steps):
            self.send(region, "z", ("cross", self.groups[abs(steps)]), to_xlo)

        def begin(self, *targets):
            self.send(r, "z", (1, "z"), *targets)

        def begin_x(self):
            self.send(r, "x", (1, "own"), to_za, to_zb)

        def cross_x(self):
            self.send(r, "x", ("x",), to_xlo)

        def cross_z(self):
            self.cross(r, 0)

        def partner(self):
            self.landed(("x",), X_ROWS)
            self.send(par_row(0), "x", (1, "other"), to_za, to_zb)

        def z_first(self, steps):
            self.landed((steps, "z"), 2 * z_rows)
            for way, target, part in ((-1, to_za, "z0"), (1, to_zb, "z1")):
                region = own_row(way * steps)
                self.send(region, part if steps == 3 else "z", (steps + 1, "z"), target)
            for way in (-1, 1):
                self.cross(own_row(way * steps), steps)

        def own(self, steps):
            self.landed((steps, "own"), 2 * X_ROWS)
            if steps < 3:
                self.send(own_row(-steps), "x", (steps + 1, "own"), to_za)
                self.send(own_row(steps), "x", (steps + 1, "own"), to_zb)
            else:
                self.send(own_row(-steps), "x", (4, "x"), to_za)

        def other(self, steps):
            self.landed((steps, "other"), 2 * X_ROWS)
            if steps < 3:
                self.send(par_row(-steps), "x", (steps + 1, "other"), to_za)
                self.send(par_row(steps), "x", (steps + 1, "other"), to_zb)
            else:
                self.send(par_row(steps), "x", (4, "x"), to_zb)

        def far_first(self):
            self.landed((4, "z"), z_rows)
            self.cross(own_row(4), 4)

        def far(self):
            self.landed((4, "x"), 2 * X_ROWS)

        def crossed(self, group):
            regions = sum((1, 2, 2, 2, 1)[d] for d in range(5) if self.groups[d] == group)
            self.landed(("cross", group), regions * z_rows)

    def cat(steps, own_xhi=True):
        return ((xhi if own_xhi else xhi2) * 4 + yat(steps)) * 2 + core

    class Row(Panel):
        def __init__(self, buf, half, x_first, y_first, groups):
            units = dict(enumerate(x_first))
            self.xf = list(units)
            self.groups = groups
            self.y_rows = 0
            if y_first:
                first, count = y_first
                self.y_rows = count
                units["y"] = (first, count)
                units["y0"] = (first, count // 2)
                units["y1"] = (first + count // 2, count // 2)
            super().__init__(buf, half, units)

        def share(self, steps, unit, own_xhi=True):
            group = self.groups[abs(steps), own_xhi]
            self.send(cat(steps, own_xhi), unit, ("sib", group), to_core)

        def sibling(self, group):
            regions = sum(2 if s == 1 else 1 for (s, _), g in self.groups.items() if g == group)
            self.landed(("sib", group), regions * REGION)

        def begin(self):
            me = cat(0)
            for u in self.xf:
                self.share(0, u)
                self.send(me, u, ("hop", u), to_xhi)
            if self.y_rows:
                self.send(me, "y", ("first",), to_yc, to_yd)
                self.send(me, "y", ("late", 0), to_xhi)
                self.share(0, "y")
            for u in self.xf:
                self.send(me, u, ("near", u), to_yc, to_yd)

        def x_hop(self, u):
            self.landed(("hop", u), self.units[u][1])
            self.send(cat(0, False), u, ("par", u), to_yc, to_yd)
            self.share(0, u, False)

        def y_near_first(self):
            self.landed(("first",), 2 * self.y_rows)
            self.send(cat(-1), "y0", ("ff",), to_yc)
            self.send(cat(1), "y1", ("ff",), to_yd)
            for way in (-1, 1):
                self.send(cat(way), "y", ("late", 1), to_xhi)
                self.share(way, "y")

        def y_near_own(self, u):
            self.landed(("near", u), 2 * self.units[u][1])
            self.send(cat(-1), u, ("far", u), to_yc)
            self.share(-1, u)
            self.share(1, u)

        def y_near_par(self, u):
            self.landed(("par", u), 2 * self.units[u][1])
            self.send(cat(1, False), u, ("far", u), to_yd)
            self.share(-1, u, False)
            self.share(1, u, False)

        def x_late(self, step):
            self.landed(("late", step), self.y_rows * (2 if step == 1 else 1))
            self.share(step, "y", False)
            if step == 1:
                self.share(-1, "y", False)

        def y_far_first(self):
            self.landed(("ff",), self.y_rows)
            self.send(cat(2), "y", ("late", 2), to_xhi)
            self.share(2, "y")

        def y_far(self, u):
            self.landed(("far", u), 2 * self.units[u][1])
            self.share(2, u)
            self.share(2, u, False)

    both = [(0, REGION // 2), (REGION // 2, REGION // 2)]
    thirds = [(s * BS, BS) for s in range(3)]
    rest = (REGION - Y_ROWS) // 2
    spots = [(s, o) for s in (0, 1, 2) for o in (True, False)]
    a = Column(0, [0, 0, 0, 0, 0])
    b = Column(1, [0, 0, 2, 3, 4])
    row = Row(rowbuf, None, thirds, None, {k: k[0] // 2 for k in spots})
    sq0 = Row(
        sqbuf, 0, both, None,
        {(0, True): 2, (0, False): 2, (1, True): 2, (1, False): 0, (2, True): 1, (2, False): 1},
    )
    sq1 = Row(
        sqbuf, 1, [(Y_ROWS, rest), (Y_ROWS + rest, rest)], (0, Y_ROWS),
        {(0, True): 0, (0, False): 1, (1, True): 2, (1, False): 3, (2, True): 4, (2, False): 4},
    )

    a.cross_x()
    a.begin(to_za, to_zb)
    a.begin_x()
    row.begin()
    a.cross_z()

    def table(p, carry):
        left = [jnp.int32(-1)] * 3
        count = jnp.int32(0)
        for b in range(16):
            here = mask[4 * r + b // 4, 4 * p + b % 4] > 0
            for l in range(3):
                left[l] = jnp.where(here & (count == l), b, left[l])
            count = count + jnp.where(here, 1, 0)
        count = jnp.int32(0)
        places = []
        for b in range(16):
            here = mask[4 * p + b // 4, 4 * c + b % 4] > 0
            places.append(jnp.where(here, count, 3))
            count = count + jnp.where(here, 1, 0)
        for q in range(3):
            own = own_ids[q]
            column = [jnp.int32(3)] * 4
            for kk in range(4):
                for b in range(4):
                    column[kk] = jnp.where(own % 4 == b, places[4 * kk + b], column[kk])
            for l in range(3):
                found = jnp.int32(3)
                for kk in range(4):
                    found = jnp.where(left[l] % 4 == kk, column[kk], found)
                good = (own >= 0) & (left[l] >= 0) & (left[l] // 4 == own // 4)
                found = jnp.where(good, found, 3)
                meets[p, 3 * q + l] = found
        return carry

    lax.fori_loop(0, 8, table, 0)

    def near_step(half):
        def step(p):
            for s in range(3):
                stage[s] = colbuf[rows_of(3 * p + s), half * LANES : (half + 1) * LANES]
            total = near_acc[half]
            for l in range(3):
                right = jnp.concatenate(
                    [stage[meets[p, 3 * q + l]] for q in range(3)], axis=1
                )
                total = total + jnp.dot(
                    rowbuf[rows_of(3 * p + l)], right, preferred_element_type=jnp.float32
                )
            near_acc[half] = total

        return step

    def far_step(half):
        def step(p):
            for s in range(3):
                far_stage[half, s] = colbuf[rows_of(3 * p + s, half * LANES, LANES)]
            left = jnp.concatenate(
                [
                    sqbuf[rows_of(3 * p + l), half * LANES : (half + 1) * LANES]
                    for l in range(3)
                ],
                axis=1,
            )
            for q in range(3):
                right = jnp.concatenate(
                    [far_stage[half, meets[p, 3 * q + l]] for l in range(3)], axis=0
                )
                acc[q] += jnp.dot(left, right, preferred_element_type=jnp.float32)

        return step

    def far_whole(p):
        for half in range(2):
            for s in range(3):
                far_stage[half, s] = colbuf[rows_of(3 * p + s, half * LANES, LANES)]
        for q in range(3):
            total = acc[q]
            for l in range(3):
                place = meets[p, 3 * q + l]
                right = jnp.concatenate([far_stage[0, place], far_stage[1, place]], axis=0)
                total = total + jnp.dot(
                    sqbuf[rows_of(3 * p + l)], right, preferred_element_type=jnp.float32
                )
            acc[q] = total

    def each(count, where, step):
        def body(i, carry):
            step(where(i))
            return carry

        lax.fori_loop(0, count, body, 0)

    def ring_region(steps):
        return lambda i: 2 * zat((1 - 2 * (i // 2)) * steps) + i % 2

    def square_out(half):
        for q in range(3):
            sqbuf[rows_of(3 * c + q), half * LANES : (half + 1) * LANES] = near_acc[
                half, :, q * LANES : (q + 1) * LANES
            ].astype(jnp.bfloat16)

    def chips_at(step):
        return lambda i: ((i // 2) * 4 + yat(step)) * 2 + i % 2

    a.z_first(1)
    a.partner()
    row.y_near_own(0)
    a.own(1)
    lax.fori_loop(8, 16, table, 0)
    row.x_hop(0)
    a.other(1)
    row.x_hop(1)
    a.z_first(2)
    a.own(2)
    row.x_hop(2)
    row.y_near_own(1)
    row.y_near_own(2)
    a.other(2)
    row.y_near_par(0)
    a.z_first(3)
    row.y_near_par(1)
    a.own(3)
    b.begin(to_zb)
    row.y_near_par(2)
    a.other(3)
    b.begin(to_za)
    b.begin_x()
    row.y_far(0)
    a.far_first()
    b.cross_x()
    b.cross_z()
    row.y_far(1)
    a.far()
    b.z_first(1)
    row.sibling(0)
    a.crossed(0)
    each(4, chips_at(0), near_step(0))
    b.partner()
    row.y_far(2)
    each(4, chips_at(1), near_step(0))
    b.own(1)
    b.z_first(2)
    each(4, chips_at(-1), near_step(0))
    row.sibling(1)
    each(4, chips_at(2), near_step(0))
    square_out(0)
    sq0.begin()
    b.other(1)
    b.crossed(0)
    each(6, lambda i: 2 * zat((i // 2 + 1) % 3 - 1) + i % 2, near_step(1))
    b.own(2)
    b.z_first(3)
    sq0.x_hop(0)
    sq0.y_near_own(0)
    b.other(2)
    sq0.x_hop(1)
    sq0.y_near_own(1)
    b.own(3)
    b.far_first()
    b.crossed(2)
    each(2, lambda i: 2 * zat(2) + i, near_step(1))
    sq0.y_near_par(0)
    each(2, lambda i: 2 * zat(-2) + i, near_step(1))
    b.other(3)
    sq0.y_near_par(1)
    b.crossed(3)
    each(4, ring_region(3), near_step(1))
    sq0.y_far(0)
    b.far()
    b.crossed(4)
    each(2, lambda i: 2 * zat(4) + i, near_step(1))
    square_out(1)
    sq1.begin()

    sq0.y_far(1)
    sq0.sibling(0)
    each(4, lambda i: (xhi2 * 4 + yat(1 - 2 * (i // 2))) * 2 + i % 2, far_step(0))
    sq0.sibling(1)
    each(4, chips_at(2), far_step(0))
    sq1.y_near_first()
    sq1.x_hop(0)
    sq1.y_near_own(0)
    sq1.x_hop(1)
    sq1.y_near_own(1)
    sq0.sibling(2)
    sq1.sibling(0)
    each(2, lambda i: (xhi * 4 + y) * 2 + i, far_whole)
    sq1.y_far_first()
    sq1.x_late(0)
    sq1.y_near_par(0)
    sq1.sibling(2)
    each(2, lambda i: (xhi * 4 + yat(1)) * 2 + i, far_whole)
    sq1.y_near_par(1)
    sq1.x_late(1)
    each(2, lambda i: (xhi * 4 + yat(-1)) * 2 + i, far_whole)
    sq1.y_far(0)
    sq1.sibling(1)
    each(2, lambda i: (xhi2 * 4 + y) * 2 + i, far_whole)
    sq1.y_far(1)
    sq1.x_late(2)
    sq1.sibling(3)
    each(4, lambda i: (xhi2 * 4 + yat(1 - 2 * (i // 2))) * 2 + i % 2, far_step(1))
    each(2, lambda i: (i * 4 + yat(2)) * 2 + core, far_step(1))
    sq1.sibling(4)
    each(2, lambda i: (i * 4 + yat(2)) * 2 + core2, far_step(1))

    tiles[3] = zero
    for q in range(3):
        value = 3.0 * sqbuf[rows_of(3 * c + q)].astype(jnp.float32) - 2.0 * acc[q]
        tiles[q] = value.astype(jnp.bfloat16)
    for s in range(3):
        out[s] = tiles[rank[s]]

    for panel in panels.values():
        panel.drain()


def local(tiles, stack, mask):
    hbm = pl.BlockSpec(memory_space=pltpu.HBM)
    result = pl.pallas_call(
        kernel,
        out_shape=jax.ShapeDtypeStruct((3, BS, BS), jnp.bfloat16),
        in_specs=[hbm, hbm, hbm],
        out_specs=pl.BlockSpec(memory_space=pltpu.VMEM),
        scratch_shapes=[
            pltpu.VMEM((4, BS, BS), jnp.bfloat16),
            pltpu.SMEM((1, 1, 3), jnp.int32),
            pltpu.SMEM((64, 64), jnp.int32),
            pltpu.VMEM((48 * BS, BS), jnp.bfloat16),
            pltpu.VMEM((48 * BS, BS), jnp.bfloat16),
            pltpu.VMEM((48 * BS, BS), jnp.bfloat16),
            pltpu.VMEM((4, BS, LANES), jnp.bfloat16),
            pltpu.VMEM((2, 4, LANES, BS), jnp.bfloat16),
            pltpu.VMEM((2, BS, 3 * LANES), jnp.float32),
            pltpu.VMEM((3, BS, BS), jnp.float32),
            pltpu.SMEM((16, 9), jnp.int32),
            pltpu.SemaphoreType.DMA((3,)),
            pltpu.SemaphoreType.DMA((5,)),
            pltpu.SemaphoreType.DMA((NAMES,)),
        ],
        compiler_params=pltpu.CompilerParams(
            collective_id=0, has_side_effects=True, vmem_limit_bytes=67043328
        ),
        name="purify",
    )(tiles[0, 0], stack, mask)
    return result[None, None]


def solution(mesh):
    placed = (P("row", "col", None, None, None), P("row", "col", None), P())
    return jax.shard_map(
        local,
        mesh=mesh,
        in_specs=placed,
        out_specs=P("row", "col", None, None, None),
        check_vma=False,
    )
```

time: 95.5 us -> 83.3 us (0.87)
  Pallas kernels: 92.2 us -> 81.4 us
  local copies, waits for them, and re-layouts: 3.16 us -> 1.77 us
    pallas_call x1, Pallas kernels: 92.2 us -> 81.4 us  [local(): pl.pallas_call(kernel, out_shape=jax.ShapeDtypeStruct((3, BS, BS), jnp.bf...]
    unnamed x7 -> x1, local copies, waits for them, and re-layouts: 3.16 us -> 1.77 us
where the time goes in v2:
time: 83.3 us; the launch traced here: 83.2 us
  Pallas kernels  81.4 us (98%)
  local copies, waits for them, and re-layouts  1.77 us (2%)
    pallas_call x1, Pallas kernels, local(): pl.pallas_call(kernel, out_shape=jax.ShapeDtypeStruct((3, BS, BS), jnp.bf...  81.4 us
    unnamed x1, local copies, waits for them, and re-layouts  1.77 us

profile of v2, /device:TPU:1, one launch (start us, length us, event | category | flops | bytes accessed | tf_op | source)
XLA Modules:
  0.0 83.2 jit_solution(11469328027577435009)
XLA Ops:
  0.0 81.4 %purify.1 = bf16[3,256,256]{2,1,0:T(8,128)(2,1)} custom-call(bf16[3,256,256]{2,1,0:T(8,128)(2,1)} %bitcast.3, s32[1,1,3]{2,1,0:T(1,128)} %stack_in.1, s32[64,64]{1,0:T(8,128)} %mask_in.1), custom_call_target="tpu_custom_call" | custom-call | tf_op jit(solution)/shard_map/purify/pallas_call | solution.py:515
  81.4 1.8 %copy.5 = bf16[1,1,3,256,256]{4,3,2,1,0:T(8,128)(2,1)} copy(bf16[1,1,3,256,256]{4,3,2,1,0:T(8,128)(2,1)} %bitcast.2) | data formatting | bytes 786432

commit v3 on v2

--- a/solution.py
+++ b/solution.py
@@ -134,6 +134,8 @@
     z_rows = REGION - X_ROWS
     col_units = {
         "x": (0, X_ROWS),
+        "x0": (0, X_ROWS // 2),
+        "x1": (X_ROWS // 2, X_ROWS // 2),
         "z": (X_ROWS, z_rows),
         "z0": (X_ROWS, z_rows // 2),
         "z1": (X_ROWS + z_rows // 2, z_rows // 2),
@@ -185,7 +187,8 @@
                 self.send(par_row(-steps), "x", (steps + 1, "other"), to_za)
                 self.send(par_row(steps), "x", (steps + 1, "other"), to_zb)
             else:
-                self.send(par_row(steps), "x", (4, "x"), to_zb)
+                self.send(par_row(steps), "x1", (4, "x"), to_zb)
+                self.send(par_row(-steps), "x0", (4, "x"), to_za)
 
         def far_first(self):
             self.landed((4, "z"), z_rows)
@@ -467,34 +470,37 @@
     square_out(1)
     sq1.begin()
 
+    sq0.sibling(2)
+    each(4, lambda i: (xhi * 4 + yat(1 - 2 * (i // 2))) * 2 + i % 2, far_step(0))
     sq0.y_far(1)
     sq0.sibling(0)
     each(4, lambda i: (xhi2 * 4 + yat(1 - 2 * (i // 2))) * 2 + i % 2, far_step(0))
-    sq0.sibling(1)
-    each(4, chips_at(2), far_step(0))
     sq1.y_near_first()
     sq1.x_hop(0)
     sq1.y_near_own(0)
+    sq0.sibling(1)
+    each(2, lambda i: (i * 4 + yat(2)) * 2 + core, far_step(0))
     sq1.x_hop(1)
     sq1.y_near_own(1)
-    sq0.sibling(2)
+    each(2, lambda i: (i * 4 + yat(2)) * 2 + core2, far_step(0))
+    sq1.y_far_first()
     sq1.sibling(0)
     each(2, lambda i: (xhi * 4 + y) * 2 + i, far_whole)
-    sq1.y_far_first()
     sq1.x_late(0)
     sq1.y_near_par(0)
     sq1.sibling(2)
-    each(2, lambda i: (xhi * 4 + yat(1)) * 2 + i, far_whole)
+    each(2, lambda i: (xhi * 4 + yat(1)) * 2 + i, far_step(1))
     sq1.y_near_par(1)
     sq1.x_late(1)
-    each(2, lambda i: (xhi * 4 + yat(-1)) * 2 + i, far_whole)
-    sq1.y_far(0)
+    each(2, lambda i: (xhi * 4 + yat(-1)) * 2 + i, far_step(1))
     sq1.sibling(1)
     each(2, lambda i: (xhi2 * 4 + y) * 2 + i, far_whole)
+    sq1.y_far(0)
+    sq1.sibling(3)
+    each(2, lambda i: (xhi2 * 4 + yat(1)) * 2 + i, far_step(1))
     sq1.y_far(1)
     sq1.x_late(2)
-    sq1.sibling(3)
-    each(4, lambda i: (xhi2 * 4 + yat(1 - 2 * (i // 2))) * 2 + i % 2, far_step(1))
+    each(2, lambda i: (xhi2 * 4 + yat(-1)) * 2 + i, far_step(1))
     each(2, lambda i: (i * 4 + yat(2)) * 2 + core, far_step(1))
     sq1.sibling(4)
     each(2, lambda i: (i * 4 + yat(2)) * 2 + core2, far_step(1))

time: 83.3 us -> 81 us (0.972)
  Pallas kernels: 81.4 us -> 79 us
    pallas_call x1, Pallas kernels: 81.4 us -> 79 us  [local(): pl.pallas_call(kernel, out_shape=jax.ShapeDtypeStruct((3, BS, BS), jnp.bf...]
where the time goes in v3:
time: 81 us; the launch traced here: 80.8 us
  Pallas kernels  79 us (98%)
  local copies, waits for them, and re-layouts  1.77 us (2%)
    pallas_call x1, Pallas kernels, local(): pl.pallas_call(kernel, out_shape=jax.ShapeDtypeStruct((3, BS, BS), jnp.bf...  79 us
    unnamed x1, local copies, waits for them, and re-layouts  1.77 us

profile of v3, /device:TPU:1, one launch (start us, length us, event | category | flops | bytes accessed | tf_op | source)
XLA Modules:
  0.0 80.8 jit_solution(4389441739404486861)
XLA Ops:
  0.0 79.0 %purify.1 = bf16[3,256,256]{2,1,0:T(8,128)(2,1)} custom-call(bf16[3,256,256]{2,1,0:T(8,128)(2,1)} %bitcast.3, s32[1,1,3]{2,1,0:T(1,128)} %stack_in.1, s32[64,64]{1,0:T(8,128)} %mask_in.1), custom_call_target="tpu_custom_call" | custom-call | tf_op jit(solution)/shard_map/purify/pallas_call | solution.py:521
  79.1 1.8 %copy.5 = bf16[1,1,3,256,256]{4,3,2,1,0:T(8,128)(2,1)} copy(bf16[1,1,3,256,256]{4,3,2,1,0:T(8,128)(2,1)} %bitcast.2) | data formatting | bytes 786432

commit v4 on v3

--- a/solution.py
+++ b/solution.py
@@ -9,7 +9,7 @@
 BS = 256
 LANES = 128
 REGION = 3 * BS
-NAMES = 72
+NAMES = 76
 X_ROWS = 448
 Y_ROWS = 320
 
@@ -281,7 +281,6 @@
 
     both = [(0, REGION // 2), (REGION // 2, REGION // 2)]
     thirds = [(s * BS, BS) for s in range(3)]
-    rest = (REGION - Y_ROWS) // 2
     spots = [(s, o) for s in (0, 1, 2) for o in (True, False)]
     a = Column(0, [0, 0, 0, 0, 0])
     b = Column(1, [0, 0, 2, 3, 4])
@@ -291,7 +290,7 @@
         {(0, True): 2, (0, False): 2, (1, True): 2, (1, False): 0, (2, True): 1, (2, False): 1},
     )
     sq1 = Row(
-        sqbuf, 1, [(Y_ROWS, rest), (Y_ROWS + rest, rest)], (0, Y_ROWS),
+        sqbuf, 1, [(320, 160), (480, 144), (624, 144)], (0, Y_ROWS),
         {(0, True): 0, (0, False): 1, (1, True): 2, (1, False): 3, (2, True): 4, (2, False): 4},
     )
 
@@ -478,10 +477,12 @@
     sq1.y_near_first()
     sq1.x_hop(0)
     sq1.y_near_own(0)
+    sq1.x_hop(1)
     sq0.sibling(1)
     each(2, lambda i: (i * 4 + yat(2)) * 2 + core, far_step(0))
-    sq1.x_hop(1)
+    sq1.x_hop(2)
     sq1.y_near_own(1)
+    sq1.y_near_own(2)
     each(2, lambda i: (i * 4 + yat(2)) * 2 + core2, far_step(0))
     sq1.y_far_first()
     sq1.sibling(0)
@@ -491,6 +492,7 @@
     sq1.sibling(2)
     each(2, lambda i: (xhi * 4 + yat(1)) * 2 + i, far_step(1))
     sq1.y_near_par(1)
+    sq1.y_near_par(2)
     sq1.x_late(1)
     each(2, lambda i: (xhi * 4 + yat(-1)) * 2 + i, far_step(1))
     sq1.sibling(1)
@@ -499,6 +501,7 @@
     sq1.sibling(3)
     each(2, lambda i: (xhi2 * 4 + yat(1)) * 2 + i, far_step(1))
     sq1.y_far(1)
+    sq1.y_far(2)
     sq1.x_late(2)
     each(2, lambda i: (xhi2 * 4 + yat(-1)) * 2 + i, far_step(1))
     each(2, lambda i: (i * 4 + yat(2)) * 2 + core, far_step(1))

time: 81 us -> 81.1 us (level)
  no operation moved by 1% of the time
where the time goes in v4:
time: 81.1 us; the launch traced here: 80.9 us
  Pallas kernels  79.1 us (98%)
  local copies, waits for them, and re-layouts  1.77 us (2%)
    pallas_call x1, Pallas kernels, local(): pl.pallas_call(kernel, out_shape=jax.ShapeDtypeStruct((3, BS, BS), jnp.bf...  79.1 us
    unnamed x1, local copies, waits for them, and re-layouts  1.77 us

profile of v4, /device:TPU:1, one launch (start us, length us, event | category | flops | bytes accessed | tf_op | source)
XLA Modules:
  0.0 80.9 jit_solution(6714553730572802963)
XLA Ops:
  0.0 79.1 %purify.1 = bf16[3,256,256]{2,1,0:T(8,128)(2,1)} custom-call(bf16[3,256,256]{2,1,0:T(8,128)(2,1)} %bitcast.3, s32[1,1,3]{2,1,0:T(1,128)} %stack_in.1, s32[64,64]{1,0:T(8,128)} %mask_in.1), custom_call_target="tpu_custom_call" | custom-call | tf_op jit(solution)/shard_map/purify/pallas_call | solution.py:524
  79.1 1.8 %copy.5 = bf16[1,1,3,256,256]{4,3,2,1,0:T(8,128)(2,1)} copy(bf16[1,1,3,256,256]{4,3,2,1,0:T(8,128)(2,1)} %bitcast.2) | data formatting | bytes 786432
